TPU v7x, 256 devices: a whole 4x4x8 slice. The times are simulated.
256 devices in a mesh: row: 8 (over z_hi, core), col: 8 (over y, z_lo), depth: 4 (over x).
Axes of the slice: x: 4, y: 4, z: 8 (z_hi: 4, z_lo: 2; z = z_hi * 2 + z_lo), core: 2. Of those that a mesh axis runs over, the one named last changes fastest.
Arguments:
- factor: float32 [32768, 1536], P(('row', 'col', 'depth')), may hold values from -1 to 4, as said below
- update: float32 [32768, 256], P(('row', 'col', 'depth')), may hold values from -0.375 to 0.375
Outputs:
- new_factor: float32 [32768, 1536], P(('row', 'col', 'depth'))
- new_update: float32 [32768, 256], P(('row', 'col', 'depth'))
Inputs may be any that keep to these rules, and one draw needn't show every extreme that they name: `factor`: zero above the diagonal; each diagonal entry is 1 or more.
All inputs are finite; a program needn't handle non-finite values.
Results may differ from a plain program's by a relative error of at most 0.00013.
Values sent between devices are 32-bit elements; how exact they have to be, the bound alone decides.
No kernel may reach another device: no remote copies, remote signals or barrier semaphores. Data moves between devices by JAX's collectives and lax.ppermute only.
A program may use at most 128 MiB of HBM per device.

v0:
```python
import jax
import jax.numpy as jnp
from jax import lax
from jax.experimental import pallas as pl
from jax.experimental.pallas import tpu as pltpu
from jax.sharding import PartitionSpec as P


B = 512
K = 256
PANELS = 3
BLK = 128
STEP = 16
NB = 6
AXES = ("row", "col", "depth")
PASSES = 6
SHARE = 16
F32 = jnp.float32


def pieces_of(x):
    terms = []
    for _ in range(2 if PASSES == 3 else 3):
        terms.append(x.astype(jnp.bfloat16))
        x = x - terms[-1].astype(F32)
    return terms


LEFT, RIGHT = ((0, 0, 1), (0, 1, 0)) if PASSES == 3 else ((0, 0, 0, 1, 1, 2), (0, 1, 2, 0, 1, 0))


def product(a, b, da, db):
    a = a if isinstance(a, list) else pieces_of(a)
    b = b if isinstance(b, list) else pieces_of(b)
    a = jnp.concatenate([a[i] for i in LEFT], da)
    b = jnp.concatenate([b[i] for i in RIGHT], db)
    return lax.dot_general(a, b, (((da,), (db,)), ((), ())), preferred_element_type=F32)


def nn(a, b):
    return product(a, b, 1, 0)


def nt(a, b):
    return product(a, b, 1, 1)


def tn(a, b):
    return product(a, b, 0, 0)


def iota(shape, dim):
    return lax.broadcasted_iota(jnp.int32, shape, dim)


def tri_inverse_128(blocks):
    r = iota((BLK, BLK), 0)
    c = iota((BLK, BLK), 1)
    inv = [jnp.where(r == c, 1.0 / jnp.where(r == c, d, 1.0), 0.0) for d in blocks]
    m = 1
    while m < BLK:
        pick = (r // (2 * m) == c // (2 * m)) & (r // m != c // m) & (r > c)
        low = [jnp.where(pick, d, 0.0) for d in blocks]
        if m == 1:
            mid = [jnp.sum(x, axis=0, keepdims=True) for x in inv]
            row = [jnp.sum(x, axis=1, keepdims=True) for x in inv]
            inv = [x - rr * l * mm for x, l, rr, mm in zip(inv, low, row, mid)]
        else:
            half = [nn(l, x) for l, x in zip(low, inv)]
            inv = [x - nn(x, h) for x, h in zip(inv, half)]
        m *= 2
    return inv


def row(x, s):
    return jnp.broadcast_to(x[s : s + 1, :], (8, BLK))


def col(x, c):
    return jnp.broadcast_to(x[:, c : c + 1], (8, BLK))


def cholesky_rows(blocks, j0):
    tiles = range(STEP // 8)
    shape = (8, BLK)
    r = iota(shape, 0)
    lane = iota(shape, 1)
    here = (lane >= j0) & (lane < j0 + STEP)
    x = [[w[8 * v : 8 * v + 8, :] for v in tiles] for w in blocks]
    part = [lane >= SHARE * i for i in range(len(blocks))]
    c = [[None] * (8 * v + 8) for v in tiles]
    for v in tiles:
        for t in range(8 * v + 8):
            both = col(x[0][v], j0 + t)
            for i in range(1, len(blocks)):
                both = jnp.where(part[i], col(x[i][v], j0 + t), both)
            c[v][t] = both
    mult = []
    roots = [None for _ in tiles]
    for t in range(STEP):
        first, s = divmod(t, 8)
        root = lax.rsqrt(row(c[first][t], s))
        recip = root * root
        m = {v: c[v][t] * recip for v in tiles if v >= first}
        m[first] = jnp.where(r > s, m[first], 0.0)
        for u in range(t + 1, STEP):
            y = row(c[u // 8][t], u % 8)
            for v in range(u // 8, len(tiles)):
                c[v][u] = c[v][u] - m[v] * y
        mult.append(m)
        roots[first] = root if s == 0 else jnp.where(r == s, root, roots[first])
    out = []
    for i, w in enumerate(x):
        rest = [jnp.where(here, jnp.where(lane == r + j0 + 8 * v, 1.0, 0.0), w[v]) for v in tiles]
        for t in range(STEP):
            first, s = divmod(t, 8)
            y = row(rest[first], s)
            for v, m in mult[t].items():
                rest[v] = rest[v] - col(m, SHARE * i) * y
        out.append(jnp.concatenate([rest[v] * col(roots[v], SHARE * i) for v in tiles], 0))
    return out


def chol_inverse_128(src, dst, count):
    c = iota((STEP, BLK), 1)
    steps = BLK // STEP
    w = [[src[i, q * STEP : (q + 1) * STEP, :] for q in range(steps)] for i in range(count)]
    for j in range(steps):
        j0 = j * STEP
        done = cholesky_rows([w[i][j] for i in range(count)], j0)
        for i, x in enumerate(done):
            dst[i, j0 : j0 + STEP, :] = jnp.where(c < j0 + STEP, x, 0.0)
            if j + 1 < steps:
                y = tn(x, x)
                here = (c >= j0) & (c < j0 + STEP)
                for q in range(j + 1, steps):
                    w[i][q] = jnp.where(here, 0.0, w[i][q]) - y[q * STEP : (q + 1) * STEP, :]


def call(kernel, mib, outs, scratch, scalars, *arrays):
    smem = pl.BlockSpec(memory_space=pltpu.SMEM)
    vmem = pl.BlockSpec(memory_space=pltpu.VMEM)
    outs = [s if isinstance(s, jax.ShapeDtypeStruct) else jax.ShapeDtypeStruct(s, F32) for s in outs]
    return pl.pallas_call(
        kernel,
        out_shape=outs,
        in_specs=[smem] + [vmem] * len(arrays),
        out_specs=[vmem] * len(outs),
        scratch_shapes=[pltpu.VMEM(s, F32) for s in scratch],
        compiler_params=pltpu.CompilerParams(vmem_limit_bytes=mib * 1024 * 1024),
    )(scalars, *arrays)


def pack_kernel(pos, f, u, p0, p1, p2, p3, left_a, left_b, u_s):
    depth, group = pos[0], pos[4]
    u_s[...] = u[...].T
    start = pl.multiple_of(group * B, B)
    for shift, out in enumerate((p0, p1, p2, p3)):
        for k in range(4):
            out[k * BLK : (k + 1) * BLK, :] = f[:, pl.ds(start + k * BLK, BLK)]
        first = pl.multiple_of(((depth + shift) % 4) * (K // 4), K // 4)
        out[4 * BLK :, :] = u_s[pl.ds(first, K // 4), :]
    left_a[...] = f[:, :B]
    left_b[...] = f[:, B : 2 * B]


def first_kernel(pos, p0, p1, p2, p3, inv_ref, v_ref, g_ref, d_s):
    depth = pos[0]
    for shift, p in enumerate((p0, p1, p2, p3)):
        slot = (depth + 4 - shift) % 4
        d_s[slot] = p[: 4 * BLK, :].reshape(4, BLK, BLK)
        v_ref[slot] = p[4 * BLK :, :]
    diag = tri_inverse_128([d_s[i, i] for i in range(4)])
    low10 = -nn(diag[1], nn(d_s[1, 0], diag[0]))
    low32 = -nn(diag[3], nn(d_s[3, 2], diag[2]))
    zero = jnp.zeros((BLK, BLK), F32)
    top = jnp.concatenate([jnp.concatenate([diag[0], zero], 1), jnp.concatenate([low10, diag[1]], 1)], 0)
    bot = jnp.concatenate([jnp.concatenate([diag[2], zero], 1), jnp.concatenate([low32, diag[3]], 1)], 0)
    below = jnp.concatenate(
        [jnp.concatenate([d_s[i, 0], d_s[i, 1]], 1) for i in (2, 3)], 0
    )
    cross = -nn(bot, nn(below, top))
    inv = jnp.concatenate(
        [
            jnp.concatenate([top, jnp.zeros((2 * BLK, 2 * BLK), F32)], 1),
            jnp.concatenate([cross, bot], 1),
        ],
        0,
    )
    terms = pieces_of(inv)
    for i, x in enumerate(terms):
        inv_ref[i] = x
    v = jnp.concatenate([v_ref[i] for i in range(4)], 1)
    g_ref[...] = jnp.where(pos[3] == 0, nt(v, terms), 0.0)


def left_product(pos, g, left, out):
    terms = pieces_of(g)
    for shift, piece in enumerate(left):
        slot = (pos[0] + 4 - shift) % 4
        out[slot] = nt(terms, piece[...])


def left0_kernel(pos, got1, got2, l0, l1, l2, l3, sum_ref, out):
    g = got1[...] + got2[...]
    sum_ref[...] = g
    left_product(pos, g, (l0, l1, l2, l3), out)


def left1_kernel(pos, g, l0, l1, l2, l3, out):
    left_product(pos, g[...], (l0, l1, l2, l3), out)


def solve(v, t, inv, out):
    for i in range(4):
        out[i] = v[i] - t[i]
    return nt(jnp.concatenate([out[i] for i in range(4)], 1), [inv[i] for i in range(3)])


def second_kernel(pos, v, t, inv, v_ref, g_ref):
    g_ref[...] = jnp.where(pos[3] == 1, solve(v, t, inv, v_ref), 0.0)


def third_kernel(pos, v, t, inv, g0, g1, keep, send, v_s):
    h = K // 8
    g2 = solve(v, t, inv, v_s)
    mine, theirs = slice(0, h), slice(h, 2 * h)
    owns, helps = pos[3] == 2, pos[3] == 10
    for ref, first, second in ((keep, mine, theirs), (send, theirs, mine)):
        for i, g in enumerate((g0, g1)):
            ref[:, i * B : (i + 1) * B] = jnp.where(helps, g[second, :], 0.0)
        ref[:, 2 * B :] = jnp.where(owns, g2[first], 0.0)


def last_kernel(pos, f, u, a0, a1, a2, a3, others, f_ref, u_ref, t_s, h_s, s_s, src, dst):
    depth, core, base = pos[0], pos[1], pos[2]
    for shift, mine in enumerate((a0, a1, a2, a3)):
        slot = (depth + 4 - shift) % 4
        t_s[slot * 2 + core] = mine[...]
        t_s[slot * 2 + 1 - core] = others[shift]
    acc = jnp.where(iota((K, K), 0) == iota((K, K), 1), 1.0, 0.0)
    v = u[...]
    for j in range(NB):
        gt = t_s[:, :, j * K : (j + 1) * K].reshape(K, K)
        acc = acc + nt(gt, gt)
        v = v - nt(f[:, j * K : (j + 1) * K], gt)
        for k in range(2):
            sl = slice(k * BLK, (k + 1) * BLK)
            h_s[j, k, 0:K, :] = acc[:, sl]
            h_s[j, k, K : K + BLK, :] = v[:, sl]
        g = gt.T
        if j == 0:
            first = g
        else:
            for k in range(2):
                h_s[j - 1, k, K + BLK :, :] = g[:, k * BLK : (k + 1) * BLK]

    def before(j):
        if j == 0:
            return u[...]
        return jnp.concatenate([h_s[j - 1, k, K : K + BLK, :] for k in range(2)], 1)

    def step(i, carry):
        del carry

        @pl.when(i == 0)
        def _():
            for j in range(NB):
                src[j] = h_s[j, 0, 0:BLK, :]

        chol_inverse_128(src, dst, NB)

        @pl.when(i == 0)
        def _():
            for j in range(NB):
                low = nt(h_s[j, 0, BLK:, :], dst[j])
                h_s[j, 0, BLK:, :] = low
                low = h_s[j, 1, BLK:, :] - nt(low, low[0:BLK, :])
                h_s[j, 1, BLK:, :] = low
                src[j] = low[0:BLK, :]

        @pl.when(i == 1)
        def _():
            for j in range(NB):
                h_s[j, 1, K:, :] = nt(h_s[j, 1, K:, :], dst[j])
            for j in range(NB):
                if j == 0:
                    g = first
                else:
                    g = jnp.concatenate([h_s[j - 1, k, K + BLK :, :] for k in range(2)], 1)
                full = nt(jnp.concatenate([g, before(j)], 0), g)
                eye = jnp.where(iota((K, K), 0) == iota((K, K), 1), 1.0, 0.0)
                s_s[j, 0:K, :] = full[0:K] + eye
                s_s[j, K:, :] = full[K:] + f[:, j * K : (j + 1) * K]
                src[j] = s_s[j, 0:BLK, 0:BLK]

        @pl.when(i == 2)
        def _():
            for j in range(NB):
                low = nt(s_s[j, BLK:, 0:BLK], dst[j])
                s_s[j, BLK:, 0:BLK] = low
                low = s_s[j, BLK:, BLK:] - nt(low, low[0:BLK, :])
                s_s[j, BLK:, BLK:] = low
                src[j] = low[0:BLK, :]

        @pl.when(i == 3)
        def _():
            rows = base + iota((BLK, BLK), 0)
            cols = iota((BLK, BLK), 1)
            for j in range(NB):
                lo = j * K
                f_ref[:, lo : lo + BLK] = jnp.where(rows >= cols + lo, s_s[j, K:, 0:BLK], 0.0)
                lo = lo + BLK
                new = nt(s_s[j, K:, BLK:], dst[j])
                f_ref[:, lo : lo + BLK] = jnp.where(rows >= cols + lo, new, 0.0)

        return 0

    lax.fori_loop(0, 4, step, 0)
    rows = base + iota((BLK, K), 0)
    out = before(2)
    for p in range(1, PANELS):
        out = jnp.where(rows >= p * B, before(2 * p + 2), out)
    u_ref[...] = out


def last_call(pos, factor, update, *pieces):
    return call(
        last_kernel,
        32,
        [factor.shape, update.shape],
        [
            (8, K // 8, PANELS * B),
            (NB, 2, K + BLK + K, BLK),
            (NB, K + BLK, K),
            (NB, BLK, BLK),
            (NB, BLK, BLK),
        ],
        pos,
        factor,
        update,
        *pieces,
    )


def device(x, y, z, core):
    return (((z // 2) * 2 + core) * 8 + y * 2 + z % 2) * 4 + x


def owner(p, x):
    return p * 4 + x


def helper(p, x):
    return (8 + p) * 4 + x


def helper_ring(shift):
    return [(helper(p, x), helper(p, (x + shift) % 4)) for p in (1, 2) for x in range(4)]


def move(value, pairs):
    return lax.ppermute(value, AXES, pairs)


def depth_ring(shift):
    return [(owner(p, x), owner(p, (x + shift) % 4)) for p in range(PANELS) for x in range(4)]


def spread_steps():
    y0, z0 = 1, 0
    y = [("y", 2), ("y", 1), ("y", 3)]
    z = [("z", 4), ("z", 2), ("z", 6)]
    plans = ((y, z, [("z", 1)]), (z, [("z", 1)], y))
    held = [[(0, 0)], [(0, 0)]]
    for stage in range(3):
        moves = []
        new = [[], []]
        for i in range(3):
            pairs = []
            for core in range(2):
                if i >= len(plans[core][stage]):
                    continue
                axis, hop = plans[core][stage][i]
                for dy, dz in held[core]:
                    to = (dy + hop, dz) if axis == "y" else (dy, dz + hop)
                    new[core].append(to)
                    for x in range(4):
                        pairs.append(
                            (
                                device(x, (y0 + dy) % 4, (z0 + dz) % 8, core),
                                device(x, (y0 + to[0]) % 4, (z0 + to[1]) % 8, core),
                            )
                        )
            moves.append(pairs)
        for core in range(2):
            held[core] += new[core]
        yield moves


def everywhere(shift):
    return [((i // 4) * 4 + i % 4, (i // 4) * 4 + (i % 4 + shift) % 4) for i in range(256)]


def partner():
    return [
        (device(x, y, z, c), device(x, y, z, 1 - c))
        for x in range(4)
        for y in range(4)
        for z in range(8)
        for c in range(2)
    ]


def steps(factor, update):
    core = lax.axis_index("row") % 2
    depth = lax.axis_index("depth")
    flat = lax.axis_index(AXES)
    pos = jnp.stack([depth, core, flat * BLK, flat // 4, jnp.minimum(flat // 4, PANELS - 1)])
    pos = pos.astype(jnp.int32)
    quarter, half = K // 4, K // 8

    packed = (4 * BLK + quarter, BLK)
    p0, p1, p2, p3, left_a, left_b = call(
        pack_kernel, 8, [packed] * 4 + [(BLK, B)] * 2, [(K, BLK)], pos, factor, update
    )
    left_a = move(left_a, [(owner(p, x), helper(p, x)) for p in (1, 2) for x in range(4)])
    left_b = move(left_b, [(owner(2, x), helper(2, x)) for x in range(4)])
    parts, lefts = [p0], [left_a]
    for s, p in ((1, p1), (2, p2), (3, p3)):
        parts.append(move(p, depth_ring(s)))
    for s in range(1, 4):
        lefts.append(move(left_a, helper_ring(s)))
    rights = [left_b]
    for s in range(1, 4):
        rights.append(move(left_b, helper_ring(s)[4:]))
    inv, v, g0 = call(
        first_kernel,
        16,
        [jax.ShapeDtypeStruct((3, B, B), jnp.bfloat16), (4, quarter, BLK), (quarter, B)],
        [(4, 4, BLK, BLK)],
        pos,
        *parts,
    )
    got1 = move(g0, [(owner(0, x), helper(1, x)) for x in range(4)])
    g0, got1 = lax.optimization_barrier((g0, got1))
    got2 = move(g0, [(owner(0, x), helper(2, x)) for x in range(4)])
    g0, t = call(
        left0_kernel, 16, [(quarter, B), (4, quarter, BLK)], [], pos, got1, got2, *lefts
    )
    t = move(t, [(helper(p, x), owner(p, x)) for p in (1, 2) for x in range(4)])
    v, g1 = call(second_kernel, 16, [(4, quarter, BLK), (quarter, B)], [], pos, v, t, inv)
    g1 = move(g1, [(owner(1, x), helper(2, x)) for x in range(4)])
    (t,) = call(left1_kernel, 16, [(4, quarter, BLK)], [], pos, g1, *rights)
    t = move(t, [(helper(2, x), owner(2, x)) for x in range(4)])
    keep, send = call(
        third_kernel, 16, [(half, PANELS * B)] * 2, [(4, quarter, BLK)], pos, v, t, inv, g0, g1
    )
    swap = [(owner(2, x), helper(2, x)) for x in range(4)]
    value = keep + move(send, swap + [(b, a) for a, b in swap])
    for moves in spread_steps():
        value = sum([move(value, pairs) for pairs in moves], value)
    mine = [value] + [move(value, everywhere(s)) for s in range(1, 4)]
    others = move(jnp.stack(mine), partner())
    return tuple(last_call(pos, factor, update, *mine, others))


def solution(mesh):
    spec = P(AXES, None)
    return jax.shard_map(
        steps, mesh=mesh, in_specs=(spec, spec), out_specs=(spec, spec), check_vma=False
    )
```

profile of v0, /device:TPU:96, one launch (start us, length us, event | category | flops | bytes accessed | tf_op | source)
XLA Modules:
  0.0 136.2 jit_solution(1871154314843816805)
XLA Ops:
  0.7 0.1 stack.38.pos
  0.7 1.1 copy-done
  1.9 0.9 copy-done.2
  2.8 0.7 shard_map.41
  3.5 0.7 collective-permute-start
  4.1 0.7 collective-permute-start.1
  4.8 0.7 collective-permute-start.2
  5.5 0.7 collective-permute-start.5
  6.2 0.0 collective-permute-done.p1
  6.2 0.0 collective-permute-done.1.p2
  6.2 0.0 collective-permute-done.2.p3
  6.2 5.7 %shard_map.42 = (bf16[3,512,512]{2,1,0:T(8,128)(2,1)S(1)}, f32[4,64,128]{2,1,0:T(8,128)S(1)}, f32[64,512]{1,0:T(8,128)S(1)}) custom-call(s32[5]{0:T(128)S(1)} %stack.38.pos, f32[576,128]{1,0:T(8,128)S(1)} %get-tuple-element.19.p0, f32[576,128]{1,0:T(8,128)S(1)} %collective-permute-done.p1, f32[576,128]{1,0:T(8,128)S(1)} %collective-permute-done.1.p2, ...), custom_call_target="tpu_custom_call" | custom-call | tf_op jit(solution)/shard_map/pallas_call | solution.py:144
  11.9 0.7 collective-permute-start.3
  12.6 0.0 collective-permute-done.5.l0
  12.6 0.7 collective-permute-start.6
  13.3 0.7 collective-permute-start.7
  14.0 0.7 collective-permute-start.8
  14.7 0.7 collective-permute-start.11
  15.4 0.7 collective-permute-start.4
  16.1 0.0 collective-permute-done.6.l1
  16.1 0.0 collective-permute-done.7.l2
  16.1 0.0 collective-permute-done.4.got2
  16.1 1.7 %shard_map.43 = (f32[64,512]{1,0:T(8,128)S(1)}, f32[4,64,128]{2,1,0:T(8,128)S(1)}) custom-call(s32[5]{0:T(128)S(1)} %stack.38.pos, f32[64,512]{1,0:T(8,128)S(1)} %collective-permute-done.3.got1, f32[64,512]{1,0:T(8,128)S(1)} %collective-permute-done.4.got2, f32[128,512]{1,0:T(8,128)S(1)} %collective-permute-done.5.l0, ...), custom_call_target="tpu_custom_call" | custom-call | tf_op jit(solution)/shard_map/pallas_call | solution.py:144
  17.8 0.7 collective-permute-start.9
  18.5 0.7 collective-permute-start.12
  19.2 0.7 collective-permute-start.13
  19.9 0.7 collective-permute-start.14
  20.6 0.0 collective-permute-done.9.t
  20.6 1.6 %shard_map.44 = (f32[4,64,128]{2,1,0:T(8,128)S(1)}, f32[64,512]{1,0:T(8,128)S(1)}) custom-call(s32[5]{0:T(128)S(1)} %stack.38.pos, f32[4,64,128]{2,1,0:T(8,128)S(1)} %get-tuple-element.23.v, f32[4,64,128]{2,1,0:T(8,128)S(1)} %collective-permute-done.9.t, bf16[3,512,512]{2,1,0:T(8,128)(2,1)S(1)} %get-tuple-element.29.inv), custom_call_target="tpu_custom_call" | custom-call | tf_op jit(solution)/shard_map/pallas_call | solution.py:144
  22.2 0.7 collective-permute-start.10
  22.9 0.0 collective-permute-done.13.l2
  22.9 0.0 collective-permute-done.14.l3
  22.9 1.7 %shard_map.45 = f32[4,64,128]{2,1,0:T(8,128)S(1)} custom-call(s32[5]{0:T(128)S(1)} %stack.38.pos, f32[64,512]{1,0:T(8,128)S(1)} %collective-permute-done.10.g.g1, f32[128,512]{1,0:T(8,128)S(1)} %collective-permute-done.11.l0, f32[128,512]{1,0:T(8,128)S(1)} %collective-permute-done.12.l1, f32[128,512]{1,0:T(8,128)S(1)} %collective-permute-done.13.l2, ...), custom_call_target="tpu_custom_call" | custom-call | tf_op jit(solution)/shard_map/pallas_call | solution.py:144
  24.6 0.7 collective-permute-start.15
  25.3 0.0 collective-permute-done.15.t
  25.3 1.6 %shard_map.46 = (f32[32,1536]{1,0:T(8,128)S(1)}, f32[32,1536]{1,0:T(8,128)S(1)}) custom-call(s32[5]{0:T(128)S(1)} %stack.38.pos, f32[4,64,128]{2,1,0:T(8,128)S(1)} %get-tuple-element.30.v, f32[4,64,128]{2,1,0:T(8,128)S(1)} %collective-permute-done.15.t, bf16[3,512,512]{2,1,0:T(8,128)(2,1)S(1)} %get-tuple-element.29.inv, f32[64,512]{1,0:T(8,128)S(1)} %get-tuple-element.33.g0, ...), custom_call_target="tpu_custom_call" | custom-call | tf_op jit(solution)/shard_map/pallas_call | solution.py:144
  26.9 0.7 collective-permute-start.16
  27.6 0.0 collective-permute-done.16
  27.7 0.7 collective-permute-start.17
  28.3 0.7 collective-permute-start.18
  29.0 0.7 collective-permute-start.19
  29.7 0.0 collective-permute-done.17
  29.7 0.0 collective-permute-done.18
  29.8 0.0 copy-start.1
  29.8 0.0 copy-start.3
  29.8 0.8 collective-permute-start.20
  30.6 0.7 collective-permute-start.21
  31.3 0.7 collective-permute-start.22
  32.0 0.0 collective-permute-done.21
  32.0 0.0 collective-permute-done.22
  32.1 1.3 collective-permute-start.23
  33.4 0.7 collective-permute-start.24
  34.0 0.7 collective-permute-start.25
  34.7 51.5 %collective-permute-done.23 = f32[32,1536]{1,0:T(8,128)S(1)} collective-permute-done((f32[32,1536]{1,0:T(8,128)S(1)}, f32[32,1536]{1,0:T(8,128)S(1)}, u32[]{:S(2)}, u32[]{:S(2)}) %collective-permute-start.23) | collective-permute-done | bytes 196640 | tf_op jit(solution)/shard_map/ppermute | solution.py:363
  86.3 0.0 collective-permute-done.25
  86.3 1.8 %collective-permute-start.26 = (f32[32,1536]{1,0:T(8,128)S(1)}, f32[32,1536]{1,0:T(8,128)S(1)}, u32[]{:S(2)}, u32[]{:S(2)}) collective-permute-start(f32[32,1536]{1,0:T(8,128)S(1)} %add_add_fusion.a0), channel_id=1, source_target_pairs={{0,1},{1,2},{2,3},{3,0},{4,5},{5,6},{6,7},{7,4},{8,9},{9,10},{10,1... | collective-permute-start | bytes 589832 | tf_op jit(solution)/shard_map/ppermute | solution.py:363
  88.1 0.3 collective-permute-start.27
  88.4 2.5 %collective-permute-start.28 = (f32[32,1536]{1,0:T(8,128)S(1)}, f32[32,1536]{1,0:T(8,128)S(1)}, u32[]{:S(2)}, u32[]{:S(2)}) collective-permute-start(f32[32,1536]{1,0:T(8,128)S(1)} %add_add_fusion.a0), channel_id=1, source_target_pairs={{0,3},{1,0},{2,1},{3,2},{4,7},{5,4},{6,5},{7,6},{8,11},{9,8},{10,9... | collective-permute-start | bytes 589832 | tf_op jit(solution)/shard_map/ppermute | solution.py:363
  90.9 7.7 %collective-permute-done.26.a1 = f32[32,1536]{1,0:T(8,128)S(1)} collective-permute-done((f32[32,1536]{1,0:T(8,128)S(1)}, f32[32,1536]{1,0:T(8,128)S(1)}, u32[]{:S(2)}, u32[]{:S(2)}) %collective-permute-start.26) | collective-permute-done | bytes 196640 | tf_op jit(solution)/shard_map/ppermute | solution.py:363
  98.6 0.6 collective-permute-done.28.a3
  99.2 0.1 pad_maximum_fusion
  99.2 0.3 collective-permute-start.29
  99.5 2.3 %collective-permute-done.29.others = f32[4,32,1536]{2,1,0:T(8,128)S(1)} collective-permute-done((f32[4,32,1536]{2,1,0:T(8,128)S(1)}, f32[4,32,1536]{2,1,0:T(8,128)S(1)}, u32[]{:S(2)}, u32[]{:S(2)}) %collective-permute-start.29) | collective-permute-done | bytes 786464 | tf_op jit(solution)/shard_map/ppermute | solution.py:363
  101.8 34.4 %shard_map.47 = (f32[128,1536]{1,0:T(8,128)}, f32[128,256]{1,0:T(8,128)}) custom-call(s32[5]{0:T(128)S(1)} %stack.38.pos, f32[128,1536]{1,0:T(8,128)S(1)} %copy-done.1, f32[128,256]{1,0:T(8,128)S(1)} %copy-done.3, f32[32,1536]{1,0:T(8,128)S(1)} %add_add_fusion.a0, f32[32,1536]{1,0:T(8,128)S(1)} %collective-permute-done.26.a1, ...), custom_call_target="tpu_custom_call" | custom-call | tf_op jit(solution)/shard_map/pallas_call | solution.py:144
  (17 shorter events, 0.2 us)
Async XLA Ops:
  0.7 1.1 copy-start
  1.9 0.9 copy-start.2
  3.5 2.8 %collective-permute-start = (f32[576,128]{1,0:T(8,128)S(1)}, f32[576,128]{1,0:T(8,128)S(1)}, u32[]{:S(2)}, u32[]{:S(2)}) collective-permute-start(f32[576,128]{1,0:T(8,128)S(1)} %get-tuple-element.20), channel_id=1, source_target_pairs={{0,1},{1,2},{2,3},{3,0},{4,5},{5,6},{6,7},{7,4},{8,9},{9,10},{10,1... | collective-permute-start | bytes 884744 | tf_op jit(solution)/shard_map/ppermute | solution.py:363
  4.1 2.1 %collective-permute-start.1 = (f32[576,128]{1,0:T(8,128)S(1)}, f32[576,128]{1,0:T(8,128)S(1)}, u32[]{:S(2)}, u32[]{:S(2)}) collective-permute-start(f32[576,128]{1,0:T(8,128)S(1)} %get-tuple-element.21), channel_id=1, source_target_pairs={{0,2},{1,3},{2,0},{3,1},{4,6},{5,7},{6,4},{7,5},{8,10},{9,11},{10,... | collective-permute-start | bytes 884744 | tf_op jit(solution)/shard_map/ppermute | solution.py:363
  4.8 1.4 %collective-permute-start.2 = (f32[576,128]{1,0:T(8,128)S(1)}, f32[576,128]{1,0:T(8,128)S(1)}, u32[]{:S(2)}, u32[]{:S(2)}) collective-permute-start(f32[576,128]{1,0:T(8,128)S(1)} %get-tuple-element.22), channel_id=1, source_target_pairs={{0,3},{1,0},{2,1},{3,2},{4,7},{5,4},{6,5},{7,6},{8,11},{9,8},{10,9... | collective-permute-start | bytes 884744 | tf_op jit(solution)/shard_map/ppermute | solution.py:363
  5.5 7.1 %collective-permute-start.5 = (f32[128,512]{1,0:T(8,128)S(1)}, f32[128,512]{1,0:T(8,128)S(1)}, u32[]{:S(2)}, u32[]{:S(2)}) collective-permute-start(f32[128,512]{1,0:T(8,128)S(1)} %get-tuple-element.27), channel_id=1, source_target_pairs={{4,36},{5,37},{6,38},{7,39},{8,40},{9,41},{10,42},{11,43}} | collective-permute-start | bytes 786440 | tf_op jit(solution)/shard_map/ppermute | solution.py:363
  11.9 3.4 %collective-permute-start.3 = (f32[64,512]{1,0:T(8,128)S(1)}, f32[64,512]{1,0:T(8,128)S(1)}, u32[]{:S(2)}, u32[]{:S(2)}) collective-permute-start(f32[64,512]{1,0:T(8,128)S(1)} %get-tuple-element.26), channel_id=1, source_target_pairs={{0,36},{1,37},{2,38},{3,39}} | collective-permute-start | bytes 393224 | tf_op jit(solution)/shard_map/ppermute | solution.py:363
  12.6 3.4 %collective-permute-start.6 = (f32[128,512]{1,0:T(8,128)S(1)}, f32[128,512]{1,0:T(8,128)S(1)}, u32[]{:S(2)}, u32[]{:S(2)}) collective-permute-start(f32[128,512]{1,0:T(8,128)S(1)} %collective-permute-done.5.l0), channel_id=1, source_target_pairs={{36,37},{37,38},{38,39},{39,36},{40,41},{41,42},{42,43},{43,40}} | collective-permute-start | bytes 786440 | tf_op jit(solution)/shard_map/ppermute | solution.py:363
  13.3 2.8 %collective-permute-start.7 = (f32[128,512]{1,0:T(8,128)S(1)}, f32[128,512]{1,0:T(8,128)S(1)}, u32[]{:S(2)}, u32[]{:S(2)}) collective-permute-start(f32[128,512]{1,0:T(8,128)S(1)} %collective-permute-done.5.l0), channel_id=1, source_target_pairs={{36,38},{37,39},{38,36},{39,37},{40,42},{41,43},{42,40},{43,41}} | collective-permute-start | bytes 786440 | tf_op jit(solution)/shard_map/ppermute | solution.py:363
  14.0 2.1 %collective-permute-start.8 = (f32[128,512]{1,0:T(8,128)S(1)}, f32[128,512]{1,0:T(8,128)S(1)}, u32[]{:S(2)}, u32[]{:S(2)}) collective-permute-start(f32[128,512]{1,0:T(8,128)S(1)} %collective-permute-done.5.l0), channel_id=1, source_target_pairs={{36,39},{37,36},{38,37},{39,38},{40,43},{41,40},{42,41},{43,42}} | collective-permute-start | bytes 786440 | tf_op jit(solution)/shard_map/ppermute | solution.py:363
  14.7 3.8 %collective-permute-start.11 = (f32[128,512]{1,0:T(8,128)S(1)}, f32[128,512]{1,0:T(8,128)S(1)}, u32[]{:S(2)}, u32[]{:S(2)}) collective-permute-start(f32[128,512]{1,0:T(8,128)S(1)} %get-tuple-element.32), channel_id=1, source_target_pairs={{8,40},{9,41},{10,42},{11,43}} | collective-permute-start | bytes 786440 | tf_op jit(solution)/shard_map/ppermute | solution.py:363
  15.4 0.7 collective-permute-start.4
  17.8 2.7 %collective-permute-start.9 = (f32[4,64,128]{2,1,0:T(8,128)S(1)}, f32[4,64,128]{2,1,0:T(8,128)S(1)}, u32[]{:S(2)}, u32[]{:S(2)}) collective-permute-start(f32[4,64,128]{2,1,0:T(8,128)S(1)} %get-tuple-element.28), channel_id=1, source_target_pairs={{36,4},{37,5},{38,6},{39,7},{40,8},{41,9},{42,10},{43,11}} | collective-permute-start | bytes 393224 | tf_op jit(solution)/shard_map/ppermute | solution.py:363
  18.5 4.3 %collective-permute-start.12 = (f32[128,512]{1,0:T(8,128)S(1)}, f32[128,512]{1,0:T(8,128)S(1)}, u32[]{:S(2)}, u32[]{:S(2)}) collective-permute-start(f32[128,512]{1,0:T(8,128)S(1)} %collective-permute-done.11.l0), channel_id=1, source_target_pairs={{40,41},{41,42},{42,43},{43,40}} | collective-permute-start | bytes 786440 | tf_op jit(solution)/shard_map/ppermute | solution.py:363
  19.2 3.7 %collective-permute-start.13 = (f32[128,512]{1,0:T(8,128)S(1)}, f32[128,512]{1,0:T(8,128)S(1)}, u32[]{:S(2)}, u32[]{:S(2)}) collective-permute-start(f32[128,512]{1,0:T(8,128)S(1)} %collective-permute-done.11.l0), channel_id=1, source_target_pairs={{40,42},{41,43},{42,40},{43,41}} | collective-permute-start | bytes 786440 | tf_op jit(solution)/shard_map/ppermute | solution.py:363
  19.9 3.0 %collective-permute-start.14 = (f32[128,512]{1,0:T(8,128)S(1)}, f32[128,512]{1,0:T(8,128)S(1)}, u32[]{:S(2)}, u32[]{:S(2)}) collective-permute-start(f32[128,512]{1,0:T(8,128)S(1)} %collective-permute-done.11.l0), channel_id=1, source_target_pairs={{40,43},{41,40},{42,41},{43,42}} | collective-permute-start | bytes 786440 | tf_op jit(solution)/shard_map/ppermute | solution.py:363
  22.2 0.7 collective-permute-start.10
  24.6 0.7 collective-permute-start.15
  26.9 0.7 collective-permute-start.16
  27.7 2.0 %collective-permute-start.17 = (f32[32,1536]{1,0:T(8,128)S(1)}, f32[32,1536]{1,0:T(8,128)S(1)}, u32[]{:S(2)}, u32[]{:S(2)}) collective-permute-start(f32[32,1536]{1,0:T(8,128)S(1)} %add.44), channel_id=1, source_target_pairs={{8,24},{9,25},{10,26},{11,27},{40,168},{41,169},{42,170},{43,171}} | collective-permute-start | bytes 589832 | tf_op jit(solution)/shard_map/ppermute | solution.py:363
  28.3 1.4 %collective-permute-start.18 = (f32[32,1536]{1,0:T(8,128)S(1)}, f32[32,1536]{1,0:T(8,128)S(1)}, u32[]{:S(2)}, u32[]{:S(2)}) collective-permute-start(f32[32,1536]{1,0:T(8,128)S(1)} %add.44), channel_id=1, source_target_pairs={{8,16},{9,17},{10,18},{11,19},{40,104},{41,105},{42,106},{43,107}} | collective-permute-start | bytes 589832 | tf_op jit(solution)/shard_map/ppermute | solution.py:363
  29.0 0.7 collective-permute-start.19
  29.8 72.0 %copy-start.1 = (f32[128,1536]{1,0:T(8,128)S(1)}, f32[128,1536]{1,0:T(8,128)}, u32[]{:S(2)}) copy-start(f32[128,1536]{1,0:T(8,128)} %f.3) | copy-start | bytes 2359300
  29.8 72.0 %copy-start.3 = (f32[128,256]{1,0:T(8,128)S(1)}, f32[128,256]{1,0:T(8,128)}, u32[]{:S(2)}) copy-start(f32[128,256]{1,0:T(8,128)} %u.3) | copy-start | bytes 393220
  29.8 2.2 %collective-permute-start.20 = (f32[32,1536]{1,0:T(8,128)S(1)}, f32[32,1536]{1,0:T(8,128)S(1)}, u32[]{:S(2)}, u32[]{:S(2)}) collective-permute-start(f32[32,1536]{1,0:T(8,128)S(1)} %add_add_fusion.2), channel_id=1, source_target_pairs={{8,136},{9,137},{10,138},{11,139},{24,152},{25,153},{26,154},{27,1... | collective-permute-start | bytes 589832 | tf_op jit(solution)/shard_map/ppermute | solution.py:363
  30.6 1.4 %collective-permute-start.21 = (f32[32,1536]{1,0:T(8,128)S(1)}, f32[32,1536]{1,0:T(8,128)S(1)}, u32[]{:S(2)}, u32[]{:S(2)}) collective-permute-start(f32[32,1536]{1,0:T(8,128)S(1)} %add_add_fusion.2), channel_id=1, source_target_pairs={{8,72},{9,73},{10,74},{11,75},{24,88},{25,89},{26,90},{27,91},{16,... | collective-permute-start | bytes 589832 | tf_op jit(solution)/shard_map/ppermute | solution.py:363
  31.3 0.7 collective-permute-start.22
  32.1 54.2 %collective-permute-start.23 = (f32[32,1536]{1,0:T(8,128)S(1)}, f32[32,1536]{1,0:T(8,128)S(1)}, u32[]{:S(2)}, u32[]{:S(2)}) collective-permute-start(f32[32,1536]{1,0:T(8,128)S(1)} %add_add_fusion.1), channel_id=1, source_target_pairs={{8,12},{9,13},{10,14},{11,15},{24,28},{25,29},{26,30},{27,31},{16,... | collective-permute-start | bytes 589832 | tf_op jit(solution)/shard_map/ppermute | solution.py:363
  33.4 52.9 %collective-permute-start.24 = (f32[32,1536]{1,0:T(8,128)S(1)}, f32[32,1536]{1,0:T(8,128)S(1)}, u32[]{:S(2)}, u32[]{:S(2)}) collective-permute-start(f32[32,1536]{1,0:T(8,128)S(1)} %add_add_fusion.1), channel_id=1, source_target_pairs={{40,48},{41,49},{42,50},{43,51},{168,176},{169,177},{170,178},{171... | collective-permute-start | bytes 589832 | tf_op jit(solution)/shard_map/ppermute | solution.py:363
  34.0 52.2 %collective-permute-start.25 = (f32[32,1536]{1,0:T(8,128)S(1)}, f32[32,1536]{1,0:T(8,128)S(1)}, u32[]{:S(2)}, u32[]{:S(2)}) collective-permute-start(f32[32,1536]{1,0:T(8,128)S(1)} %add_add_fusion.1), channel_id=1, source_target_pairs={{40,32},{41,33},{42,34},{43,35},{168,160},{169,161},{170,162},{171... | collective-permute-start | bytes 589832 | tf_op jit(solution)/shard_map/ppermute | solution.py:363
  86.3 12.2 %collective-permute-start.26 = (f32[32,1536]{1,0:T(8,128)S(1)}, f32[32,1536]{1,0:T(8,128)S(1)}, u32[]{:S(2)}, u32[]{:S(2)}) collective-permute-start(f32[32,1536]{1,0:T(8,128)S(1)} %add_add_fusion.a0), channel_id=1, source_target_pairs={{0,1},{1,2},{2,3},{3,0},{4,5},{5,6},{6,7},{7,4},{8,9},{9,10},{10,1... | collective-permute-start | bytes 589832 | tf_op jit(solution)/shard_map/ppermute | solution.py:363
  88.1 10.4 %collective-permute-start.27 = (f32[32,1536]{1,0:T(8,128)S(1)}, f32[32,1536]{1,0:T(8,128)S(1)}, u32[]{:S(2)}, u32[]{:S(2)}) collective-permute-start(f32[32,1536]{1,0:T(8,128)S(1)} %add_add_fusion.a0), channel_id=1, source_target_pairs={{0,2},{1,3},{2,0},{3,1},{4,6},{5,7},{6,4},{7,5},{8,10},{9,11},{10,... | collective-permute-start | bytes 589832 | tf_op jit(solution)/shard_map/ppermute | solution.py:363
  88.4 10.8 %collective-permute-start.28 = (f32[32,1536]{1,0:T(8,128)S(1)}, f32[32,1536]{1,0:T(8,128)S(1)}, u32[]{:S(2)}, u32[]{:S(2)}) collective-permute-start(f32[32,1536]{1,0:T(8,128)S(1)} %add_add_fusion.a0), channel_id=1, source_target_pairs={{0,3},{1,0},{2,1},{3,2},{4,7},{5,4},{6,5},{7,6},{8,11},{9,8},{10,9... | collective-permute-start | bytes 589832 | tf_op jit(solution)/shard_map/ppermute | solution.py:363
  99.2 2.6 %collective-permute-start.29 = (f32[4,32,1536]{2,1,0:T(8,128)S(1)}, f32[4,32,1536]{2,1,0:T(8,128)S(1)}, u32[]{:S(2)}, u32[]{:S(2)}) collective-permute-start(f32[4,32,1536]{2,1,0:T(8,128)S(1)} %pad_maximum_fusion), channel_id=1, source_target_pairs={{0,32},{32,0},{4,36},{36,4},{64,96},{96,64},{68,100},{100,68},{128... | collective-permute-start | bytes 2359304 | tf_op jit(solution)/shard_map/ppermute | solution.py:363
where the time goes:
time: 137 us; the launch traced here: 136 us
  waiting for transfers between devices  62.2 us (45%)
  Pallas kernels  47.4 us (35%)
  starting transfers between devices  23.1 us (17%)
  local copies, waits for them, and re-layouts  2.14 us (2%)
    ppermute x30, waiting for transfers between devices, move(): return lax.ppermute(value, AXES, pairs)  62.2 us
    pallas_call x7, Pallas kernels, call(): pl.pallas_call(kernel, out_shape=outs, in_specs=[smem] + [vmem] * len(arr...  47.4 us
    ppermute x30, starting transfers between devices, move(): return lax.ppermute(value, AXES, pairs)  23.1 us
  transfers between devices with their start and end apart: 30, of which 4 were waited for; matrix products, arithmetic and copies ran while one was open for 0% of the time, Pallas kernels for 7%

commit v1 on v0

--- a/solution.py
+++ b/solution.py
@@ -165,33 +165,35 @@
 
 
 def first_kernel(pos, p0, p1, p2, p3, inv_ref, v_ref, g_ref, d_s):
-    depth = pos[0]
-    for shift, p in enumerate((p0, p1, p2, p3)):
-        slot = (depth + 4 - shift) % 4
-        d_s[slot] = p[: 4 * BLK, :].reshape(4, BLK, BLK)
-        v_ref[slot] = p[4 * BLK :, :]
-    diag = tri_inverse_128([d_s[i, i] for i in range(4)])
-    low10 = -nn(diag[1], nn(d_s[1, 0], diag[0]))
-    low32 = -nn(diag[3], nn(d_s[3, 2], diag[2]))
-    zero = jnp.zeros((BLK, BLK), F32)
-    top = jnp.concatenate([jnp.concatenate([diag[0], zero], 1), jnp.concatenate([low10, diag[1]], 1)], 0)
-    bot = jnp.concatenate([jnp.concatenate([diag[2], zero], 1), jnp.concatenate([low32, diag[3]], 1)], 0)
-    below = jnp.concatenate(
-        [jnp.concatenate([d_s[i, 0], d_s[i, 1]], 1) for i in (2, 3)], 0
-    )
-    cross = -nn(bot, nn(below, top))
-    inv = jnp.concatenate(
-        [
-            jnp.concatenate([top, jnp.zeros((2 * BLK, 2 * BLK), F32)], 1),
-            jnp.concatenate([cross, bot], 1),
-        ],
-        0,
-    )
-    terms = pieces_of(inv)
-    for i, x in enumerate(terms):
-        inv_ref[i] = x
-    v = jnp.concatenate([v_ref[i] for i in range(4)], 1)
-    g_ref[...] = jnp.where(pos[3] == 0, nt(v, terms), 0.0)
+    @pl.when(pos[3] < PANELS)
+    def _():
+        depth = pos[0]
+        for shift, p in enumerate((p0, p1, p2, p3)):
+            slot = (depth + 4 - shift) % 4
+            d_s[slot] = p[: 4 * BLK, :].reshape(4, BLK, BLK)
+            v_ref[slot] = p[4 * BLK :, :]
+        diag = tri_inverse_128([d_s[i, i] for i in range(4)])
+        low10 = -nn(diag[1], nn(d_s[1, 0], diag[0]))
+        low32 = -nn(diag[3], nn(d_s[3, 2], diag[2]))
+        zero = jnp.zeros((BLK, BLK), F32)
+        top = jnp.concatenate([jnp.concatenate([diag[0], zero], 1), jnp.concatenate([low10, diag[1]], 1)], 0)
+        bot = jnp.concatenate([jnp.concatenate([diag[2], zero], 1), jnp.concatenate([low32, diag[3]], 1)], 0)
+        below = jnp.concatenate(
+            [jnp.concatenate([d_s[i, 0], d_s[i, 1]], 1) for i in (2, 3)], 0
+        )
+        cross = -nn(bot, nn(below, top))
+        inv = jnp.concatenate(
+            [
+                jnp.concatenate([top, jnp.zeros((2 * BLK, 2 * BLK), F32)], 1),
+                jnp.concatenate([cross, bot], 1),
+            ],
+            0,
+        )
+        terms = pieces_of(inv)
+        for i, x in enumerate(terms):
+            inv_ref[i] = x
+        v = jnp.concatenate([v_ref[i] for i in range(4)], 1)
+        g_ref[...] = nt(v, terms)
 
 
 def left_product(pos, g, left, out):
@@ -202,13 +204,17 @@
 
 
 def left0_kernel(pos, got1, got2, l0, l1, l2, l3, sum_ref, out):
-    g = got1[...] + got2[...]
-    sum_ref[...] = g
-    left_product(pos, g, (l0, l1, l2, l3), out)
+    @pl.when((pos[3] == 9) | (pos[3] == 10))
+    def _():
+        g = got1[...] + got2[...]
+        sum_ref[...] = g
+        left_product(pos, g, (l0, l1, l2, l3), out)
 
 
 def left1_kernel(pos, g, l0, l1, l2, l3, out):
-    left_product(pos, g[...], (l0, l1, l2, l3), out)
+    @pl.when(pos[3] == 10)
+    def _():
+        left_product(pos, g[...], (l0, l1, l2, l3), out)
 
 
 def solve(v, t, inv, out):
@@ -218,18 +224,29 @@
 
 
 def second_kernel(pos, v, t, inv, v_ref, g_ref):
-    g_ref[...] = jnp.where(pos[3] == 1, solve(v, t, inv, v_ref), 0.0)
+    @pl.when((pos[3] == 1) | (pos[3] == 2))
+    def _():
+        g_ref[...] = solve(v, t, inv, v_ref)
 
 
 def third_kernel(pos, v, t, inv, g0, g1, keep, send, v_s):
     h = K // 8
-    g2 = solve(v, t, inv, v_s)
     mine, theirs = slice(0, h), slice(h, 2 * h)
     owns, helps = pos[3] == 2, pos[3] == 10
-    for ref, first, second in ((keep, mine, theirs), (send, theirs, mine)):
-        for i, g in enumerate((g0, g1)):
-            ref[:, i * B : (i + 1) * B] = jnp.where(helps, g[second, :], 0.0)
-        ref[:, 2 * B :] = jnp.where(owns, g2[first], 0.0)
+    for ref in (keep, send):
+        ref[...] = jnp.zeros((h, PANELS * B), F32)
+
+    @pl.when(helps)
+    def _():
+        for ref, rows in ((keep, theirs), (send, mine)):
+            for i, g in enumerate((g0, g1)):
+                ref[:, i * B : (i + 1) * B] = g[rows, :]
+
+    @pl.when(owns)
+    def _():
+        g2 = solve(v, t, inv, v_s)
+        keep[:, 2 * B :] = g2[mine]
+        send[:, 2 * B :] = g2[theirs]
 
 
 def last_kernel(pos, f, u, a0, a1, a2, a3, others, f_ref, u_ref, t_s, h_s, s_s, src, dst):

time: 137 us -> 136 us (level)
  Pallas kernels: 47.4 us -> 37.8 us
  waiting for transfers between devices: 62.2 us -> 70.7 us
    pallas_call x7, Pallas kernels: 47.4 us -> 37.8 us  [call(): pl.pallas_call(kernel, out_shape=outs, in_specs=[smem] + [vmem] * len(arr...]
    ppermute x30, waiting for transfers between devices: 62.2 us -> 70.7 us  [move(): return lax.ppermute(value, AXES, pairs)]
  transfers between devices with their start and end apart: 30 -> 30, of which waited for: 4 -> 4; matrix products, arithmetic and copies ran while one was open for 0% -> 0% of each run, Pallas kernels for 7% -> 1%
where the time goes in v1:
time: 136 us; the launch traced here: 135 us
  waiting for transfers between devices  70.7 us (52%)
  Pallas kernels  37.8 us (28%)
  starting transfers between devices  23.1 us (17%)
  local copies, waits for them, and re-layouts  2.14 us (2%)
    ppermute x30, waiting for transfers between devices, move(): return lax.ppermute(value, AXES, pairs)  70.7 us
    pallas_call x7, Pallas kernels, call(): pl.pallas_call(kernel, out_shape=outs, in_specs=[smem] + [vmem] * len(arr...  37.8 us
    ppermute x30, starting transfers between devices, move(): return lax.ppermute(value, AXES, pairs)  23.1 us
  transfers between devices with their start and end apart: 30, of which 4 were waited for; matrix products, arithmetic and copies ran while one was open for 0% of the time, Pallas kernels for 1%

profile of v1, /device:TPU:96, one launch (start us, length us, event | category | flops | bytes accessed | tf_op | source)
XLA Modules:
  0.0 135.2 jit_solution(5630906793521107052)
XLA Ops:
  0.7 0.1 stack.38.pos
  0.7 1.1 copy-done
  1.9 0.9 copy-done.2
  2.8 0.7 shard_map.41
  3.5 0.7 collective-permute-start
  4.1 0.7 collective-permute-start.1
  4.8 0.7 collective-permute-start.2
  5.5 0.7 collective-permute-start.5
  6.2 0.0 collective-permute-done.p1
  6.2 0.0 collective-permute-done.1.p2
  6.2 0.0 collective-permute-done.2.p3
  6.2 0.6 shard_map.42
  6.8 0.7 collective-permute-start.3
  7.5 0.0 collective-permute-done.5.l0
  7.5 0.7 collective-permute-start.6
  8.2 0.7 collective-permute-start.7
  8.8 0.7 collective-permute-start.8
  9.5 0.7 collective-permute-start.11
  10.2 0.0 collective-permute-done.3.got1
  10.2 0.7 collective-permute-start.4
  10.9 0.0 collective-permute-done.6.l1
  10.9 0.0 collective-permute-done.7.l2
  10.9 0.0 collective-permute-done.4.got2
  10.9 0.6 shard_map.43
  11.5 0.7 collective-permute-start.9
  12.2 0.0 collective-permute-done.11.l0
  12.2 0.7 collective-permute-start.12
  12.9 0.7 collective-permute-start.13
  13.6 0.7 collective-permute-start.14
  14.3 0.6 shard_map.44
  14.8 0.7 collective-permute-start.10
  15.5 0.0 collective-permute-done.12.l1
  15.5 0.0 collective-permute-done.14.l3
  15.5 0.0 collective-permute-done.10.g.g1
  15.5 0.6 shard_map.45
  16.1 0.7 collective-permute-start.15
  16.8 0.6 shard_map.46
  17.4 0.7 collective-permute-start.16
  18.0 0.0 collective-permute-done.16
  18.1 0.7 collective-permute-start.17
  18.8 0.7 collective-permute-start.18
  19.5 0.7 collective-permute-start.19
  20.1 0.0 collective-permute-done.17
  20.2 0.0 copy-start.1
  20.2 0.0 copy-start.3
  20.2 0.8 collective-permute-start.20
  21.0 0.7 collective-permute-start.21
  21.7 0.7 collective-permute-start.22
  22.4 0.0 collective-permute-done.21
  22.5 1.3 collective-permute-start.23
  23.8 0.7 collective-permute-start.24
  24.5 0.7 collective-permute-start.25
  25.2 60.1 %collective-permute-done.23 = f32[32,1536]{1,0:T(8,128)S(1)} collective-permute-done((f32[32,1536]{1,0:T(8,128)S(1)}, f32[32,1536]{1,0:T(8,128)S(1)}, u32[]{:S(2)}, u32[]{:S(2)}) %collective-permute-start.23) | collective-permute-done | bytes 196640 | tf_op jit(solution)/shard_map/ppermute | solution.py:380
  85.3 0.0 collective-permute-done.24
  85.3 1.8 %collective-permute-start.26 = (f32[32,1536]{1,0:T(8,128)S(1)}, f32[32,1536]{1,0:T(8,128)S(1)}, u32[]{:S(2)}, u32[]{:S(2)}) collective-permute-start(f32[32,1536]{1,0:T(8,128)S(1)} %add_add_fusion.a0), channel_id=1, source_target_pairs={{0,1},{1,2},{2,3},{3,0},{4,5},{5,6},{6,7},{7,4},{8,9},{9,10},{10,1... | collective-permute-start | bytes 589832 | tf_op jit(solution)/shard_map/ppermute | solution.py:380
  87.1 0.3 collective-permute-start.27
  87.4 2.5 %collective-permute-start.28 = (f32[32,1536]{1,0:T(8,128)S(1)}, f32[32,1536]{1,0:T(8,128)S(1)}, u32[]{:S(2)}, u32[]{:S(2)}) collective-permute-start(f32[32,1536]{1,0:T(8,128)S(1)} %add_add_fusion.a0), channel_id=1, source_target_pairs={{0,3},{1,0},{2,1},{3,2},{4,7},{5,4},{6,5},{7,6},{8,11},{9,8},{10,9... | collective-permute-start | bytes 589832 | tf_op jit(solution)/shard_map/ppermute | solution.py:380
  89.9 7.7 %collective-permute-done.26.a1 = f32[32,1536]{1,0:T(8,128)S(1)} collective-permute-done((f32[32,1536]{1,0:T(8,128)S(1)}, f32[32,1536]{1,0:T(8,128)S(1)}, u32[]{:S(2)}, u32[]{:S(2)}) %collective-permute-start.26) | collective-permute-done | bytes 196640 | tf_op jit(solution)/shard_map/ppermute | solution.py:380
  97.5 0.0 collective-permute-done.27.a2
  97.6 0.6 collective-permute-done.28.a3
  98.2 0.1 pad_maximum_fusion
  98.2 0.3 collective-permute-start.29
  98.5 2.3 %collective-permute-done.29.others = f32[4,32,1536]{2,1,0:T(8,128)S(1)} collective-permute-done((f32[4,32,1536]{2,1,0:T(8,128)S(1)}, f32[4,32,1536]{2,1,0:T(8,128)S(1)}, u32[]{:S(2)}, u32[]{:S(2)}) %collective-permute-start.29) | collective-permute-done | bytes 786464 | tf_op jit(solution)/shard_map/ppermute | solution.py:380
  100.8 34.4 %shard_map.47 = (f32[128,1536]{1,0:T(8,128)}, f32[128,256]{1,0:T(8,128)}) custom-call(s32[5]{0:T(128)S(1)} %stack.38.pos, f32[128,1536]{1,0:T(8,128)S(1)} %copy-done.1, f32[128,256]{1,0:T(8,128)S(1)} %copy-done.3, f32[32,1536]{1,0:T(8,128)S(1)} %add_add_fusion.a0, f32[32,1536]{1,0:T(8,128)S(1)} %collective-permute-done.26.a1, ...), custom_call_target="tpu_custom_call" | custom-call | tf_op jit(solution)/shard_map/pallas_call | solution.py:144
  (17 shorter events, 0.2 us)
Async XLA Ops:
  0.7 1.1 copy-start
  1.9 0.9 copy-start.2
  3.5 2.8 %collective-permute-start = (f32[576,128]{1,0:T(8,128)S(1)}, f32[576,128]{1,0:T(8,128)S(1)}, u32[]{:S(2)}, u32[]{:S(2)}) collective-permute-start(f32[576,128]{1,0:T(8,128)S(1)} %get-tuple-element.20), channel_id=1, source_target_pairs={{0,1},{1,2},{2,3},{3,0},{4,5},{5,6},{6,7},{7,4},{8,9},{9,10},{10,1... | collective-permute-start | bytes 884744 | tf_op jit(solution)/shard_map/ppermute | solution.py:380
  4.1 2.1 %collective-permute-start.1 = (f32[576,128]{1,0:T(8,128)S(1)}, f32[576,128]{1,0:T(8,128)S(1)}, u32[]{:S(2)}, u32[]{:S(2)}) collective-permute-start(f32[576,128]{1,0:T(8,128)S(1)} %get-tuple-element.21), channel_id=1, source_target_pairs={{0,2},{1,3},{2,0},{3,1},{4,6},{5,7},{6,4},{7,5},{8,10},{9,11},{10,... | collective-permute-start | bytes 884744 | tf_op jit(solution)/shard_map/ppermute | solution.py:380
  4.8 1.4 %collective-permute-start.2 = (f32[576,128]{1,0:T(8,128)S(1)}, f32[576,128]{1,0:T(8,128)S(1)}, u32[]{:S(2)}, u32[]{:S(2)}) collective-permute-start(f32[576,128]{1,0:T(8,128)S(1)} %get-tuple-element.22), channel_id=1, source_target_pairs={{0,3},{1,0},{2,1},{3,2},{4,7},{5,4},{6,5},{7,6},{8,11},{9,8},{10,9... | collective-permute-start | bytes 884744 | tf_op jit(solution)/shard_map/ppermute | solution.py:380
  5.5 2.0 %collective-permute-start.5 = (f32[128,512]{1,0:T(8,128)S(1)}, f32[128,512]{1,0:T(8,128)S(1)}, u32[]{:S(2)}, u32[]{:S(2)}) collective-permute-start(f32[128,512]{1,0:T(8,128)S(1)} %get-tuple-element.27), channel_id=1, source_target_pairs={{4,36},{5,37},{6,38},{7,39},{8,40},{9,41},{10,42},{11,43}} | collective-permute-start | bytes 786440 | tf_op jit(solution)/shard_map/ppermute | solution.py:380
  6.8 3.4 %collective-permute-start.3 = (f32[64,512]{1,0:T(8,128)S(1)}, f32[64,512]{1,0:T(8,128)S(1)}, u32[]{:S(2)}, u32[]{:S(2)}) collective-permute-start(f32[64,512]{1,0:T(8,128)S(1)} %get-tuple-element.26), channel_id=1, source_target_pairs={{0,36},{1,37},{2,38},{3,39}} | collective-permute-start | bytes 393224 | tf_op jit(solution)/shard_map/ppermute | solution.py:380
  7.5 3.4 %collective-permute-start.6 = (f32[128,512]{1,0:T(8,128)S(1)}, f32[128,512]{1,0:T(8,128)S(1)}, u32[]{:S(2)}, u32[]{:S(2)}) collective-permute-start(f32[128,512]{1,0:T(8,128)S(1)} %collective-permute-done.5.l0), channel_id=1, source_target_pairs={{36,37},{37,38},{38,39},{39,36},{40,41},{41,42},{42,43},{43,40}} | collective-permute-start | bytes 786440 | tf_op jit(solution)/shard_map/ppermute | solution.py:380
  8.2 2.8 %collective-permute-start.7 = (f32[128,512]{1,0:T(8,128)S(1)}, f32[128,512]{1,0:T(8,128)S(1)}, u32[]{:S(2)}, u32[]{:S(2)}) collective-permute-start(f32[128,512]{1,0:T(8,128)S(1)} %collective-permute-done.5.l0), channel_id=1, source_target_pairs={{36,38},{37,39},{38,36},{39,37},{40,42},{41,43},{42,40},{43,41}} | collective-permute-start | bytes 786440 | tf_op jit(solution)/shard_map/ppermute | solution.py:380
  8.8 2.1 %collective-permute-start.8 = (f32[128,512]{1,0:T(8,128)S(1)}, f32[128,512]{1,0:T(8,128)S(1)}, u32[]{:S(2)}, u32[]{:S(2)}) collective-permute-start(f32[128,512]{1,0:T(8,128)S(1)} %collective-permute-done.5.l0), channel_id=1, source_target_pairs={{36,39},{37,36},{38,37},{39,38},{40,43},{41,40},{42,41},{43,42}} | collective-permute-start | bytes 786440 | tf_op jit(solution)/shard_map/ppermute | solution.py:380
  9.5 2.7 %collective-permute-start.11 = (f32[128,512]{1,0:T(8,128)S(1)}, f32[128,512]{1,0:T(8,128)S(1)}, u32[]{:S(2)}, u32[]{:S(2)}) collective-permute-start(f32[128,512]{1,0:T(8,128)S(1)} %get-tuple-element.32), channel_id=1, source_target_pairs={{8,40},{9,41},{10,42},{11,43}} | collective-permute-start | bytes 786440 | tf_op jit(solution)/shard_map/ppermute | solution.py:380
  10.2 0.7 collective-permute-start.4
  11.5 2.7 %collective-permute-start.9 = (f32[4,64,128]{2,1,0:T(8,128)S(1)}, f32[4,64,128]{2,1,0:T(8,128)S(1)}, u32[]{:S(2)}, u32[]{:S(2)}) collective-permute-start(f32[4,64,128]{2,1,0:T(8,128)S(1)} %get-tuple-element.28), channel_id=1, source_target_pairs={{36,4},{37,5},{38,6},{39,7},{40,8},{41,9},{42,10},{43,11}} | collective-permute-start | bytes 393224 | tf_op jit(solution)/shard_map/ppermute | solution.py:380
  12.2 3.3 %collective-permute-start.12 = (f32[128,512]{1,0:T(8,128)S(1)}, f32[128,512]{1,0:T(8,128)S(1)}, u32[]{:S(2)}, u32[]{:S(2)}) collective-permute-start(f32[128,512]{1,0:T(8,128)S(1)} %collective-permute-done.11.l0), channel_id=1, source_target_pairs={{40,41},{41,42},{42,43},{43,40}} | collective-permute-start | bytes 786440 | tf_op jit(solution)/shard_map/ppermute | solution.py:380
  12.9 2.6 %collective-permute-start.13 = (f32[128,512]{1,0:T(8,128)S(1)}, f32[128,512]{1,0:T(8,128)S(1)}, u32[]{:S(2)}, u32[]{:S(2)}) collective-permute-start(f32[128,512]{1,0:T(8,128)S(1)} %collective-permute-done.11.l0), channel_id=1, source_target_pairs={{40,42},{41,43},{42,40},{43,41}} | collective-permute-start | bytes 786440 | tf_op jit(solution)/shard_map/ppermute | solution.py:380
  13.6 2.0 %collective-permute-start.14 = (f32[128,512]{1,0:T(8,128)S(1)}, f32[128,512]{1,0:T(8,128)S(1)}, u32[]{:S(2)}, u32[]{:S(2)}) collective-permute-start(f32[128,512]{1,0:T(8,128)S(1)} %collective-permute-done.11.l0), channel_id=1, source_target_pairs={{40,43},{41,40},{42,41},{43,42}} | collective-permute-start | bytes 786440 | tf_op jit(solution)/shard_map/ppermute | solution.py:380
  14.8 0.7 collective-permute-start.10
  16.1 0.7 collective-permute-start.15
  17.4 0.7 collective-permute-start.16
  18.1 2.0 %collective-permute-start.17 = (f32[32,1536]{1,0:T(8,128)S(1)}, f32[32,1536]{1,0:T(8,128)S(1)}, u32[]{:S(2)}, u32[]{:S(2)}) collective-permute-start(f32[32,1536]{1,0:T(8,128)S(1)} %add.44), channel_id=1, source_target_pairs={{8,24},{9,25},{10,26},{11,27},{40,168},{41,169},{42,170},{43,171}} | collective-permute-start | bytes 589832 | tf_op jit(solution)/shard_map/ppermute | solution.py:380
  18.8 1.4 %collective-permute-start.18 = (f32[32,1536]{1,0:T(8,128)S(1)}, f32[32,1536]{1,0:T(8,128)S(1)}, u32[]{:S(2)}, u32[]{:S(2)}) collective-permute-start(f32[32,1536]{1,0:T(8,128)S(1)} %add.44), channel_id=1, source_target_pairs={{8,16},{9,17},{10,18},{11,19},{40,104},{41,105},{42,106},{43,107}} | collective-permute-start | bytes 589832 | tf_op jit(solution)/shard_map/ppermute | solution.py:380
  19.5 0.7 collective-permute-start.19
  20.2 80.6 %copy-start.1 = (f32[128,1536]{1,0:T(8,128)S(1)}, f32[128,1536]{1,0:T(8,128)}, u32[]{:S(2)}) copy-start(f32[128,1536]{1,0:T(8,128)} %f.3) | copy-start | bytes 2359300
  20.2 80.6 %copy-start.3 = (f32[128,256]{1,0:T(8,128)S(1)}, f32[128,256]{1,0:T(8,128)}, u32[]{:S(2)}) copy-start(f32[128,256]{1,0:T(8,128)} %u.3) | copy-start | bytes 393220
  20.2 2.2 %collective-permute-start.20 = (f32[32,1536]{1,0:T(8,128)S(1)}, f32[32,1536]{1,0:T(8,128)S(1)}, u32[]{:S(2)}, u32[]{:S(2)}) collective-permute-start(f32[32,1536]{1,0:T(8,128)S(1)} %add_add_fusion.2), channel_id=1, source_target_pairs={{8,136},{9,137},{10,138},{11,139},{24,152},{25,153},{26,154},{27,1... | collective-permute-start | bytes 589832 | tf_op jit(solution)/shard_map/ppermute | solution.py:380
  21.0 1.4 %collective-permute-start.21 = (f32[32,1536]{1,0:T(8,128)S(1)}, f32[32,1536]{1,0:T(8,128)S(1)}, u32[]{:S(2)}, u32[]{:S(2)}) collective-permute-start(f32[32,1536]{1,0:T(8,128)S(1)} %add_add_fusion.2), channel_id=1, source_target_pairs={{8,72},{9,73},{10,74},{11,75},{24,88},{25,89},{26,90},{27,91},{16,... | collective-permute-start | bytes 589832 | tf_op jit(solution)/shard_map/ppermute | solution.py:380
  21.7 0.7 collective-permute-start.22
  22.5 62.8 %collective-permute-start.23 = (f32[32,1536]{1,0:T(8,128)S(1)}, f32[32,1536]{1,0:T(8,128)S(1)}, u32[]{:S(2)}, u32[]{:S(2)}) collective-permute-start(f32[32,1536]{1,0:T(8,128)S(1)} %add_add_fusion.1), channel_id=1, source_target_pairs={{8,12},{9,13},{10,14},{11,15},{24,28},{25,29},{26,30},{27,31},{16,... | collective-permute-start | bytes 589832 | tf_op jit(solution)/shard_map/ppermute | solution.py:380
  23.8 61.5 %collective-permute-start.24 = (f32[32,1536]{1,0:T(8,128)S(1)}, f32[32,1536]{1,0:T(8,128)S(1)}, u32[]{:S(2)}, u32[]{:S(2)}) collective-permute-start(f32[32,1536]{1,0:T(8,128)S(1)} %add_add_fusion.1), channel_id=1, source_target_pairs={{40,48},{41,49},{42,50},{43,51},{168,176},{169,177},{170,178},{171... | collective-permute-start | bytes 589832 | tf_op jit(solution)/shard_map/ppermute | solution.py:380
  24.5 60.8 %collective-permute-start.25 = (f32[32,1536]{1,0:T(8,128)S(1)}, f32[32,1536]{1,0:T(8,128)S(1)}, u32[]{:S(2)}, u32[]{:S(2)}) collective-permute-start(f32[32,1536]{1,0:T(8,128)S(1)} %add_add_fusion.1), channel_id=1, source_target_pairs={{40,32},{41,33},{42,34},{43,35},{168,160},{169,161},{170,162},{171... | collective-permute-start | bytes 589832 | tf_op jit(solution)/shard_map/ppermute | solution.py:380
  85.3 12.2 %collective-permute-start.26 = (f32[32,1536]{1,0:T(8,128)S(1)}, f32[32,1536]{1,0:T(8,128)S(1)}, u32[]{:S(2)}, u32[]{:S(2)}) collective-permute-start(f32[32,1536]{1,0:T(8,128)S(1)} %add_add_fusion.a0), channel_id=1, source_target_pairs={{0,1},{1,2},{2,3},{3,0},{4,5},{5,6},{6,7},{7,4},{8,9},{9,10},{10,1... | collective-permute-start | bytes 589832 | tf_op jit(solution)/shard_map/ppermute | solution.py:380
  87.1 10.4 %collective-permute-start.27 = (f32[32,1536]{1,0:T(8,128)S(1)}, f32[32,1536]{1,0:T(8,128)S(1)}, u32[]{:S(2)}, u32[]{:S(2)}) collective-permute-start(f32[32,1536]{1,0:T(8,128)S(1)} %add_add_fusion.a0), channel_id=1, source_target_pairs={{0,2},{1,3},{2,0},{3,1},{4,6},{5,7},{6,4},{7,5},{8,10},{9,11},{10,... | collective-permute-start | bytes 589832 | tf_op jit(solution)/shard_map/ppermute | solution.py:380
  87.4 10.8 %collective-permute-start.28 = (f32[32,1536]{1,0:T(8,128)S(1)}, f32[32,1536]{1,0:T(8,128)S(1)}, u32[]{:S(2)}, u32[]{:S(2)}) collective-permute-start(f32[32,1536]{1,0:T(8,128)S(1)} %add_add_fusion.a0), channel_id=1, source_target_pairs={{0,3},{1,0},{2,1},{3,2},{4,7},{5,4},{6,5},{7,6},{8,11},{9,8},{10,9... | collective-permute-start | bytes 589832 | tf_op jit(solution)/shard_map/ppermute | solution.py:380
  98.2 2.6 %collective-permute-start.29 = (f32[4,32,1536]{2,1,0:T(8,128)S(1)}, f32[4,32,1536]{2,1,0:T(8,128)S(1)}, u32[]{:S(2)}, u32[]{:S(2)}) collective-permute-start(f32[4,32,1536]{2,1,0:T(8,128)S(1)} %pad_maximum_fusion), channel_id=1, source_target_pairs={{0,32},{32,0},{4,36},{36,4},{64,96},{96,64},{68,100},{100,68},{128... | collective-permute-start | bytes 2359304 | tf_op jit(solution)/shard_map/ppermute | solution.py:380

commit v2 on v1

--- a/solution.py
+++ b/solution.py
@@ -1,3 +1,5 @@
+from functools import partial
+
 import jax
 import jax.numpy as jnp
 from jax import lax
@@ -196,25 +198,24 @@
         g_ref[...] = nt(v, terms)
 
 
-def left_product(pos, g, left, out):
+def left_product(pos, g, left, out, base=None):
     terms = pieces_of(g)
     for shift, piece in enumerate(left):
         slot = (pos[0] + 4 - shift) % 4
-        out[slot] = nt(terms, piece[...])
-
-
-def left0_kernel(pos, got1, got2, l0, l1, l2, l3, sum_ref, out):
-    @pl.when((pos[3] == 9) | (pos[3] == 10))
-    def _():
-        g = got1[...] + got2[...]
-        sum_ref[...] = g
-        left_product(pos, g, (l0, l1, l2, l3), out)
-
-
-def left1_kernel(pos, g, l0, l1, l2, l3, out):
+        new = nt(terms, piece[...])
+        out[slot] = new if base is None else base[slot] + new
+
+
+def left_kernel(group, pos, g, l0, l1, l2, l3, out):
+    @pl.when(pos[3] == group)
+    def _():
+        left_product(pos, g[...], (l0, l1, l2, l3), out)
+
+
+def left_add_kernel(pos, g, t, l0, l1, l2, l3, out):
     @pl.when(pos[3] == 10)
     def _():
-        left_product(pos, g[...], (l0, l1, l2, l3), out)
+        left_product(pos, g[...], (l0, l1, l2, l3), out, t)
 
 
 def solve(v, t, inv, out):
@@ -223,10 +224,10 @@
     return nt(jnp.concatenate([out[i] for i in range(4)], 1), [inv[i] for i in range(3)])
 
 
-def second_kernel(pos, v, t, inv, v_ref, g_ref):
-    @pl.when((pos[3] == 1) | (pos[3] == 2))
-    def _():
-        g_ref[...] = solve(v, t, inv, v_ref)
+def second_kernel(pos, v, t, inv, g_ref, v_s):
+    @pl.when(pos[3] == 1)
+    def _():
+        g_ref[...] = solve(v, t, inv, v_s)
 
 
 def third_kernel(pos, v, t, inv, g0, g1, keep, send, v_s):
@@ -462,16 +463,16 @@
     got1 = move(g0, [(owner(0, x), helper(1, x)) for x in range(4)])
     g0, got1 = lax.optimization_barrier((g0, got1))
     got2 = move(g0, [(owner(0, x), helper(2, x)) for x in range(4)])
-    g0, t = call(
-        left0_kernel, 16, [(quarter, B), (4, quarter, BLK)], [], pos, got1, got2, *lefts
-    )
-    t = move(t, [(helper(p, x), owner(p, x)) for p in (1, 2) for x in range(4)])
-    v, g1 = call(second_kernel, 16, [(4, quarter, BLK), (quarter, B)], [], pos, v, t, inv)
+    slots = (4, quarter, BLK)
+    (t,) = call(partial(left_kernel, 9), 16, [slots], [], pos, got1, *lefts)
+    t = move(t, [(helper(1, x), owner(1, x)) for x in range(4)])
+    (g1,) = call(second_kernel, 16, [(quarter, B)], [slots], pos, v, t, inv)
     g1 = move(g1, [(owner(1, x), helper(2, x)) for x in range(4)])
-    (t,) = call(left1_kernel, 16, [(4, quarter, BLK)], [], pos, g1, *rights)
+    (t,) = call(partial(left_kernel, 10), 16, [slots], [], pos, got2, *lefts)
+    (t,) = call(left_add_kernel, 16, [slots], [], pos, g1, t, *rights)
     t = move(t, [(helper(2, x), owner(2, x)) for x in range(4)])
     keep, send = call(
-        third_kernel, 16, [(half, PANELS * B)] * 2, [(4, quarter, BLK)], pos, v, t, inv, g0, g1
+        third_kernel, 16, [(half, PANELS * B)] * 2, [(4, quarter, BLK)], pos, v, t, inv, got2, g1
     )
     swap = [(owner(2, x), helper(2, x)) for x in range(4)]
     value = keep + move(send, swap + [(b, a) for a, b in swap])

time: 136 us -> 128 us (0.941)
  waiting for transfers between devices: 70.7 us -> 62.4 us
    ppermute x30, waiting for transfers between devices: 70.7 us -> 62.4 us  [move(): return lax.ppermute(value, AXES, pairs)]
    pallas_call x7 -> x8, Pallas kernels: 37.8 us -> 38.6 us  [call(): pl.pallas_call(kernel, out_shape=outs, in_specs=[smem] + [vmem] * len(arr...]
  transfers between devices with their start and end apart: 30 -> 30, of which waited for: 4 -> 4; matrix products, arithmetic and copies ran while one was open for 0% -> 0% of each run, Pallas kernels for 1% -> 2%
where the time goes in v2:
time: 128 us; the launch traced here: 127 us
  waiting for transfers between devices  62.4 us (49%)
  Pallas kernels  38.6 us (30%)
  starting transfers between devices  23 us (18%)
  local copies, waits for them, and re-layouts  2.14 us (2%)
    ppermute x30, waiting for transfers between devices, move(): return lax.ppermute(value, AXES, pairs)  62.4 us
    pallas_call x8, Pallas kernels, call(): pl.pallas_call(kernel, out_shape=outs, in_specs=[smem] + [vmem] * len(arr...  38.6 us
    ppermute x30, starting transfers between devices, move(): return lax.ppermute(value, AXES, pairs)  23 us
  transfers between devices with their start and end apart: 30, of which 4 were waited for; matrix products, arithmetic and copies ran while one was open for 0% of the time, Pallas kernels for 2%

profile of v2, /device:TPU:96, one launch (start us, length us, event | category | flops | bytes accessed | tf_op | source)
XLA Modules:
  0.0 127.5 jit_solution(13985121188015064887)
XLA Ops:
  0.7 0.1 stack.38.pos
  0.7 1.1 copy-done
  1.9 0.9 copy-done.2
  2.8 0.7 shard_map.41
  3.5 0.7 collective-permute-start
  4.1 0.7 collective-permute-start.1
  4.8 0.7 collective-permute-start.4
  5.5 0.7 collective-permute-start.2
  6.2 0.7 collective-permute-start.5
  6.9 0.7 collective-permute-start.6
  7.6 0.0 collective-permute-done.p1
  7.6 0.7 collective-permute-start.7
  8.3 0.7 collective-permute-start.11
  9.0 0.0 collective-permute-done.2.p3
  9.0 0.6 shard_map.42
  9.5 0.7 collective-permute-start.3
  10.2 0.0 collective-permute-done.5.l1
  10.2 0.0 collective-permute-done.6.l2
  10.3 0.6 shard_map.43
  10.8 0.7 collective-permute-start.8
  11.5 0.0 collective-permute-done.11.l0
  11.5 0.7 collective-permute-start.12
  12.2 0.7 collective-permute-start.13
  12.9 0.7 collective-permute-start.14
  13.6 0.7 collective-permute-start.10
  14.2 0.0 collective-permute-done.8.t
  14.3 0.6 shard_map.44
  14.8 0.7 collective-permute-start.9
  15.5 0.0 collective-permute-done.10.g.g0
  15.5 0.6 shard_map.45.t
  16.1 0.0 collective-permute-done.12.l1
  16.1 0.0 collective-permute-done.14.l3
  16.1 0.0 collective-permute-done.9.g.g1
  16.1 0.6 shard_map.46
  16.7 0.7 collective-permute-start.15
  17.3 0.6 shard_map.47
  17.9 0.7 collective-permute-start.16
  18.6 0.0 collective-permute-done.16
  18.6 0.7 collective-permute-start.17
  19.3 0.7 collective-permute-start.18
  20.0 0.7 collective-permute-start.19
  20.7 0.0 collective-permute-done.17
  20.7 0.0 collective-permute-done.19
  20.8 0.0 copy-start.1
  20.8 0.0 copy-start.3
  20.8 0.8 collective-permute-start.20
  21.6 0.7 collective-permute-start.21
  22.3 0.7 collective-permute-start.22
  23.0 0.0 collective-permute-done.20
  23.0 0.0 collective-permute-done.21
  23.0 1.3 %collective-permute-start.23 = (f32[32,1536]{1,0:T(8,128)S(1)}, f32[32,1536]{1,0:T(8,128)S(1)}, u32[]{:S(2)}, u32[]{:S(2)}) collective-permute-start(f32[32,1536]{1,0:T(8,128)S(1)} %add_add_fusion.1), channel_id=1, source_target_pairs={{8,12},{9,13},{10,14},{11,15},{24,28},{25,29},{26,30},{27,31},{16,... | collective-permute-start | bytes 589832 | tf_op jit(solution)/shard_map/ppermute | solution.py:381
  24.3 0.7 collective-permute-start.24
  25.0 0.7 collective-permute-start.25
  25.7 51.8 %collective-permute-done.23 = f32[32,1536]{1,0:T(8,128)S(1)} collective-permute-done((f32[32,1536]{1,0:T(8,128)S(1)}, f32[32,1536]{1,0:T(8,128)S(1)}, u32[]{:S(2)}, u32[]{:S(2)}) %collective-permute-start.23) | collective-permute-done | bytes 196640 | tf_op jit(solution)/shard_map/ppermute | solution.py:381
  77.5 0.0 collective-permute-done.24
  77.6 1.8 %collective-permute-start.26 = (f32[32,1536]{1,0:T(8,128)S(1)}, f32[32,1536]{1,0:T(8,128)S(1)}, u32[]{:S(2)}, u32[]{:S(2)}) collective-permute-start(f32[32,1536]{1,0:T(8,128)S(1)} %add_add_fusion.a0), channel_id=1, source_target_pairs={{0,1},{1,2},{2,3},{3,0},{4,5},{5,6},{6,7},{7,4},{8,9},{9,10},{10,1... | collective-permute-start | bytes 589832 | tf_op jit(solution)/shard_map/ppermute | solution.py:381
  79.4 0.3 collective-permute-start.27
  79.7 2.5 %collective-permute-start.28 = (f32[32,1536]{1,0:T(8,128)S(1)}, f32[32,1536]{1,0:T(8,128)S(1)}, u32[]{:S(2)}, u32[]{:S(2)}) collective-permute-start(f32[32,1536]{1,0:T(8,128)S(1)} %add_add_fusion.a0), channel_id=1, source_target_pairs={{0,3},{1,0},{2,1},{3,2},{4,7},{5,4},{6,5},{7,6},{8,11},{9,8},{10,9... | collective-permute-start | bytes 589832 | tf_op jit(solution)/shard_map/ppermute | solution.py:381
  82.2 7.7 %collective-permute-done.26.a1 = f32[32,1536]{1,0:T(8,128)S(1)} collective-permute-done((f32[32,1536]{1,0:T(8,128)S(1)}, f32[32,1536]{1,0:T(8,128)S(1)}, u32[]{:S(2)}, u32[]{:S(2)}) %collective-permute-start.26) | collective-permute-done | bytes 196640 | tf_op jit(solution)/shard_map/ppermute | solution.py:381
  89.8 0.6 collective-permute-done.28.a3
  90.4 0.1 pad_maximum_fusion
  90.5 0.1 collective-permute-start.29
  90.6 2.3 %collective-permute-done.29.others = f32[4,32,1536]{2,1,0:T(8,128)S(1)} collective-permute-done((f32[4,32,1536]{2,1,0:T(8,128)S(1)}, f32[4,32,1536]{2,1,0:T(8,128)S(1)}, u32[]{:S(2)}, u32[]{:S(2)}) %collective-permute-start.29) | collective-permute-done | bytes 786464 | tf_op jit(solution)/shard_map/ppermute | solution.py:381
  92.9 34.6 %shard_map.48 = (f32[128,1536]{1,0:T(8,128)}, f32[128,256]{1,0:T(8,128)}) custom-call(s32[5]{0:T(128)S(1)} %stack.38.pos, f32[128,1536]{1,0:T(8,128)S(1)} %copy-done.1, f32[128,256]{1,0:T(8,128)S(1)} %copy-done.3, f32[32,1536]{1,0:T(8,128)S(1)} %add_add_fusion.a0, f32[32,1536]{1,0:T(8,128)S(1)} %collective-permute-done.26.a1, ...), custom_call_target="tpu_custom_call" | custom-call | tf_op jit(solution)/shard_map/pallas_call | solution.py:146
  (18 shorter events, 0.2 us)
Async XLA Ops:
  0.7 1.1 copy-start
  1.9 0.9 copy-start.2
  3.5 4.1 %collective-permute-start = (f32[576,128]{1,0:T(8,128)S(1)}, f32[576,128]{1,0:T(8,128)S(1)}, u32[]{:S(2)}, u32[]{:S(2)}) collective-permute-start(f32[576,128]{1,0:T(8,128)S(1)} %get-tuple-element.16), channel_id=1, source_target_pairs={{0,1},{1,2},{2,3},{3,0},{4,5},{5,6},{6,7},{7,4},{8,9},{9,10},{10,1... | collective-permute-start | bytes 884744 | tf_op jit(solution)/shard_map/ppermute | solution.py:381
  4.1 4.1 %collective-permute-start.1 = (f32[576,128]{1,0:T(8,128)S(1)}, f32[576,128]{1,0:T(8,128)S(1)}, u32[]{:S(2)}, u32[]{:S(2)}) collective-permute-start(f32[576,128]{1,0:T(8,128)S(1)} %get-tuple-element.17), channel_id=1, source_target_pairs={{0,2},{1,3},{2,0},{3,1},{4,6},{5,7},{6,4},{7,5},{8,10},{9,11},{10,... | collective-permute-start | bytes 884744 | tf_op jit(solution)/shard_map/ppermute | solution.py:381
  4.8 1.4 %collective-permute-start.4 = (f32[128,512]{1,0:T(8,128)S(1)}, f32[128,512]{1,0:T(8,128)S(1)}, u32[]{:S(2)}, u32[]{:S(2)}) collective-permute-start(f32[128,512]{1,0:T(8,128)S(1)} %get-tuple-element.22), channel_id=1, source_target_pairs={{4,36},{5,37},{6,38},{7,39},{8,40},{9,41},{10,42},{11,43}} | collective-permute-start | bytes 786440 | tf_op jit(solution)/shard_map/ppermute | solution.py:381
  5.5 3.5 %collective-permute-start.2 = (f32[576,128]{1,0:T(8,128)S(1)}, f32[576,128]{1,0:T(8,128)S(1)}, u32[]{:S(2)}, u32[]{:S(2)}) collective-permute-start(f32[576,128]{1,0:T(8,128)S(1)} %get-tuple-element.18), channel_id=1, source_target_pairs={{0,3},{1,0},{2,1},{3,2},{4,7},{5,4},{6,5},{7,6},{8,11},{9,8},{10,9... | collective-permute-start | bytes 884744 | tf_op jit(solution)/shard_map/ppermute | solution.py:381
  6.2 4.0 %collective-permute-start.5 = (f32[128,512]{1,0:T(8,128)S(1)}, f32[128,512]{1,0:T(8,128)S(1)}, u32[]{:S(2)}, u32[]{:S(2)}) collective-permute-start(f32[128,512]{1,0:T(8,128)S(1)} %collective-permute-done.4.l0), channel_id=1, source_target_pairs={{36,37},{37,38},{38,39},{39,36},{40,41},{41,42},{42,43},{43,40}} | collective-permute-start | bytes 786440 | tf_op jit(solution)/shard_map/ppermute | solution.py:381
  6.9 3.3 %collective-permute-start.6 = (f32[128,512]{1,0:T(8,128)S(1)}, f32[128,512]{1,0:T(8,128)S(1)}, u32[]{:S(2)}, u32[]{:S(2)}) collective-permute-start(f32[128,512]{1,0:T(8,128)S(1)} %collective-permute-done.4.l0), channel_id=1, source_target_pairs={{36,38},{37,39},{38,36},{39,37},{40,42},{41,43},{42,40},{43,41}} | collective-permute-start | bytes 786440 | tf_op jit(solution)/shard_map/ppermute | solution.py:381
  7.6 2.7 %collective-permute-start.7 = (f32[128,512]{1,0:T(8,128)S(1)}, f32[128,512]{1,0:T(8,128)S(1)}, u32[]{:S(2)}, u32[]{:S(2)}) collective-permute-start(f32[128,512]{1,0:T(8,128)S(1)} %collective-permute-done.4.l0), channel_id=1, source_target_pairs={{36,39},{37,36},{38,37},{39,38},{40,43},{41,40},{42,41},{43,42}} | collective-permute-start | bytes 786440 | tf_op jit(solution)/shard_map/ppermute | solution.py:381
  8.3 3.2 %collective-permute-start.11 = (f32[128,512]{1,0:T(8,128)S(1)}, f32[128,512]{1,0:T(8,128)S(1)}, u32[]{:S(2)}, u32[]{:S(2)}) collective-permute-start(f32[128,512]{1,0:T(8,128)S(1)} %get-tuple-element.25), channel_id=1, source_target_pairs={{8,40},{9,41},{10,42},{11,43}} | collective-permute-start | bytes 786440 | tf_op jit(solution)/shard_map/ppermute | solution.py:381
  9.5 0.7 collective-permute-start.3
  10.8 3.4 %collective-permute-start.8 = (f32[4,64,128]{2,1,0:T(8,128)S(1)}, f32[4,64,128]{2,1,0:T(8,128)S(1)}, u32[]{:S(2)}, u32[]{:S(2)}) collective-permute-start(f32[4,64,128]{2,1,0:T(8,128)S(1)} %shard_map.43), channel_id=1, source_target_pairs={{36,4},{37,5},{38,6},{39,7}} | collective-permute-start | bytes 393224 | tf_op jit(solution)/shard_map/ppermute | solution.py:381
  11.5 4.5 %collective-permute-start.12 = (f32[128,512]{1,0:T(8,128)S(1)}, f32[128,512]{1,0:T(8,128)S(1)}, u32[]{:S(2)}, u32[]{:S(2)}) collective-permute-start(f32[128,512]{1,0:T(8,128)S(1)} %collective-permute-done.11.l0), channel_id=1, source_target_pairs={{40,41},{41,42},{42,43},{43,40}} | collective-permute-start | bytes 786440 | tf_op jit(solution)/shard_map/ppermute | solution.py:381
  12.2 3.9 %collective-permute-start.13 = (f32[128,512]{1,0:T(8,128)S(1)}, f32[128,512]{1,0:T(8,128)S(1)}, u32[]{:S(2)}, u32[]{:S(2)}) collective-permute-start(f32[128,512]{1,0:T(8,128)S(1)} %collective-permute-done.11.l0), channel_id=1, source_target_pairs={{40,42},{41,43},{42,40},{43,41}} | collective-permute-start | bytes 786440 | tf_op jit(solution)/shard_map/ppermute | solution.py:381
  12.9 3.2 %collective-permute-start.14 = (f32[128,512]{1,0:T(8,128)S(1)}, f32[128,512]{1,0:T(8,128)S(1)}, u32[]{:S(2)}, u32[]{:S(2)}) collective-permute-start(f32[128,512]{1,0:T(8,128)S(1)} %collective-permute-done.11.l0), channel_id=1, source_target_pairs={{40,43},{41,40},{42,41},{43,42}} | collective-permute-start | bytes 786440 | tf_op jit(solution)/shard_map/ppermute | solution.py:381
  13.6 1.9 %collective-permute-start.10 = (f32[64,512]{1,0:T(8,128)S(1)}, f32[64,512]{1,0:T(8,128)S(1)}, u32[]{:S(2)}, u32[]{:S(2)}) collective-permute-start(f32[64,512]{1,0:T(8,128)S(1)} %get-tuple-element.24), channel_id=1, source_target_pairs={{0,40},{1,41},{2,42},{3,43}} | collective-permute-start | bytes 393224 | tf_op jit(solution)/shard_map/ppermute | solution.py:381
  14.8 1.3 %collective-permute-start.9 = (f32[64,512]{1,0:T(8,128)S(1)}, f32[64,512]{1,0:T(8,128)S(1)}, u32[]{:S(2)}, u32[]{:S(2)}) collective-permute-start(f32[64,512]{1,0:T(8,128)S(1)} %shard_map.44), channel_id=1, source_target_pairs={{4,40},{5,41},{6,42},{7,43}} | collective-permute-start | bytes 393224 | tf_op jit(solution)/shard_map/ppermute | solution.py:381
  16.7 0.7 collective-permute-start.15
  17.9 0.7 collective-permute-start.16
  18.6 2.0 %collective-permute-start.17 = (f32[32,1536]{1,0:T(8,128)S(1)}, f32[32,1536]{1,0:T(8,128)S(1)}, u32[]{:S(2)}, u32[]{:S(2)}) collective-permute-start(f32[32,1536]{1,0:T(8,128)S(1)} %add.44), channel_id=1, source_target_pairs={{8,24},{9,25},{10,26},{11,27},{40,168},{41,169},{42,170},{43,171}} | collective-permute-start | bytes 589832 | tf_op jit(solution)/shard_map/ppermute | solution.py:381
  19.3 1.4 %collective-permute-start.18 = (f32[32,1536]{1,0:T(8,128)S(1)}, f32[32,1536]{1,0:T(8,128)S(1)}, u32[]{:S(2)}, u32[]{:S(2)}) collective-permute-start(f32[32,1536]{1,0:T(8,128)S(1)} %add.44), channel_id=1, source_target_pairs={{8,16},{9,17},{10,18},{11,19},{40,104},{41,105},{42,106},{43,107}} | collective-permute-start | bytes 589832 | tf_op jit(solution)/shard_map/ppermute | solution.py:381
  20.0 0.7 collective-permute-start.19
  20.8 72.1 %copy-start.1 = (f32[128,1536]{1,0:T(8,128)S(1)}, f32[128,1536]{1,0:T(8,128)}, u32[]{:S(2)}) copy-start(f32[128,1536]{1,0:T(8,128)} %f.3) | copy-start | bytes 2359300
  20.8 72.1 %copy-start.3 = (f32[128,256]{1,0:T(8,128)S(1)}, f32[128,256]{1,0:T(8,128)}, u32[]{:S(2)}) copy-start(f32[128,256]{1,0:T(8,128)} %u.3) | copy-start | bytes 393220
  20.8 2.2 %collective-permute-start.20 = (f32[32,1536]{1,0:T(8,128)S(1)}, f32[32,1536]{1,0:T(8,128)S(1)}, u32[]{:S(2)}, u32[]{:S(2)}) collective-permute-start(f32[32,1536]{1,0:T(8,128)S(1)} %add_add_fusion.2), channel_id=1, source_target_pairs={{8,136},{9,137},{10,138},{11,139},{24,152},{25,153},{26,154},{27,1... | collective-permute-start | bytes 589832 | tf_op jit(solution)/shard_map/ppermute | solution.py:381
  21.6 1.4 %collective-permute-start.21 = (f32[32,1536]{1,0:T(8,128)S(1)}, f32[32,1536]{1,0:T(8,128)S(1)}, u32[]{:S(2)}, u32[]{:S(2)}) collective-permute-start(f32[32,1536]{1,0:T(8,128)S(1)} %add_add_fusion.2), channel_id=1, source_target_pairs={{8,72},{9,73},{10,74},{11,75},{24,88},{25,89},{26,90},{27,91},{16,... | collective-permute-start | bytes 589832 | tf_op jit(solution)/shard_map/ppermute | solution.py:381
  22.3 0.7 collective-permute-start.22
  23.0 54.5 %collective-permute-start.23 = (f32[32,1536]{1,0:T(8,128)S(1)}, f32[32,1536]{1,0:T(8,128)S(1)}, u32[]{:S(2)}, u32[]{:S(2)}) collective-permute-start(f32[32,1536]{1,0:T(8,128)S(1)} %add_add_fusion.1), channel_id=1, source_target_pairs={{8,12},{9,13},{10,14},{11,15},{24,28},{25,29},{26,30},{27,31},{16,... | collective-permute-start | bytes 589832 | tf_op jit(solution)/shard_map/ppermute | solution.py:381
  24.3 53.2 %collective-permute-start.24 = (f32[32,1536]{1,0:T(8,128)S(1)}, f32[32,1536]{1,0:T(8,128)S(1)}, u32[]{:S(2)}, u32[]{:S(2)}) collective-permute-start(f32[32,1536]{1,0:T(8,128)S(1)} %add_add_fusion.1), channel_id=1, source_target_pairs={{40,48},{41,49},{42,50},{43,51},{168,176},{169,177},{170,178},{171... | collective-permute-start | bytes 589832 | tf_op jit(solution)/shard_map/ppermute | solution.py:381
  25.0 52.5 %collective-permute-start.25 = (f32[32,1536]{1,0:T(8,128)S(1)}, f32[32,1536]{1,0:T(8,128)S(1)}, u32[]{:S(2)}, u32[]{:S(2)}) collective-permute-start(f32[32,1536]{1,0:T(8,128)S(1)} %add_add_fusion.1), channel_id=1, source_target_pairs={{40,32},{41,33},{42,34},{43,35},{168,160},{169,161},{170,162},{171... | collective-permute-start | bytes 589832 | tf_op jit(solution)/shard_map/ppermute | solution.py:381
  77.6 12.2 %collective-permute-start.26 = (f32[32,1536]{1,0:T(8,128)S(1)}, f32[32,1536]{1,0:T(8,128)S(1)}, u32[]{:S(2)}, u32[]{:S(2)}) collective-permute-start(f32[32,1536]{1,0:T(8,128)S(1)} %add_add_fusion.a0), channel_id=1, source_target_pairs={{0,1},{1,2},{2,3},{3,0},{4,5},{5,6},{6,7},{7,4},{8,9},{9,10},{10,1... | collective-permute-start | bytes 589832 | tf_op jit(solution)/shard_map/ppermute | solution.py:381
  79.4 10.4 %collective-permute-start.27 = (f32[32,1536]{1,0:T(8,128)S(1)}, f32[32,1536]{1,0:T(8,128)S(1)}, u32[]{:S(2)}, u32[]{:S(2)}) collective-permute-start(f32[32,1536]{1,0:T(8,128)S(1)} %add_add_fusion.a0), channel_id=1, source_target_pairs={{0,2},{1,3},{2,0},{3,1},{4,6},{5,7},{6,4},{7,5},{8,10},{9,11},{10,... | collective-permute-start | bytes 589832 | tf_op jit(solution)/shard_map/ppermute | solution.py:381
  79.7 10.8 %collective-permute-start.28 = (f32[32,1536]{1,0:T(8,128)S(1)}, f32[32,1536]{1,0:T(8,128)S(1)}, u32[]{:S(2)}, u32[]{:S(2)}) collective-permute-start(f32[32,1536]{1,0:T(8,128)S(1)} %add_add_fusion.a0), channel_id=1, source_target_pairs={{0,3},{1,0},{2,1},{3,2},{4,7},{5,4},{6,5},{7,6},{8,11},{9,8},{10,9... | collective-permute-start | bytes 589832 | tf_op jit(solution)/shard_map/ppermute | solution.py:381
  90.5 2.4 %collective-permute-start.29 = (f32[4,32,1536]{2,1,0:T(8,128)S(1)}, f32[4,32,1536]{2,1,0:T(8,128)S(1)}, u32[]{:S(2)}, u32[]{:S(2)}) collective-permute-start(f32[4,32,1536]{2,1,0:T(8,128)S(1)} %pad_maximum_fusion), channel_id=1, source_target_pairs={{0,32},{32,0},{4,36},{36,4},{64,96},{96,64},{68,100},{100,68},{128... | collective-permute-start | bytes 2359304 | tf_op jit(solution)/shard_map/ppermute | solution.py:381

commit v3 on v2

--- a/solution.py
+++ b/solution.py
@@ -153,27 +153,49 @@
     )(scalars, *arrays)
 
 
-def pack_kernel(pos, f, u, p0, p1, p2, p3, left_a, left_b, u_s):
+def pack_kernel(pos, f, u, own, up, down, left_a, left_b, u_s):
     depth, group = pos[0], pos[4]
     u_s[...] = u[...].T
     start = pl.multiple_of(group * B, B)
-    for shift, out in enumerate((p0, p1, p2, p3)):
-        for k in range(4):
-            out[k * BLK : (k + 1) * BLK, :] = f[:, pl.ds(start + k * BLK, BLK)]
-        first = pl.multiple_of(((depth + shift) % 4) * (K // 4), K // 4)
-        out[4 * BLK :, :] = u_s[pl.ds(first, K // 4), :]
+    quarter, half, h = K // 4, K // 8, 2 * BLK
+
+    def cut(k):
+        return f[:, pl.ds(start + k * BLK, BLK)]
+
+    def update_rows(shift, first, size):
+        at = pl.multiple_of(((depth + shift) % 4) * quarter + first, size)
+        return u_s[pl.ds(at, size), :]
+
+    for out, order, shift, first in ((up, (0, 1, 2, 3), 1, 0), (down, (2, 3, 0, 1), 3, half)):
+        out[0:BLK, :] = cut(order[0])
+        out[BLK:h, :] = cut(order[1])
+        out[h : h + half, :] = update_rows(2, first, half)
+        out[h + half : h + half + BLK, :] = cut(order[2])
+        out[h + half + BLK : 2 * h + half, :] = cut(order[3])
+        out[2 * h + half :, :] = update_rows(shift, 0, quarter)
+    for k in range(4):
+        own[k * BLK : (k + 1) * BLK, :] = cut(k)
+    own[2 * h :, :] = update_rows(0, 0, quarter)
     left_a[...] = f[:, :B]
     left_b[...] = f[:, B : 2 * B]
 
 
-def first_kernel(pos, p0, p1, p2, p3, inv_ref, v_ref, g_ref, d_s):
+def first_kernel(pos, own, low, high, far_low, far_high, inv_ref, v_ref, g_ref, d_s):
     @pl.when(pos[3] < PANELS)
     def _():
         depth = pos[0]
-        for shift, p in enumerate((p0, p1, p2, p3)):
-            slot = (depth + 4 - shift) % 4
-            d_s[slot] = p[: 4 * BLK, :].reshape(4, BLK, BLK)
-            v_ref[slot] = p[4 * BLK :, :]
+        h, half = 2 * BLK, K // 8
+        two = (2, BLK, BLK)
+        d_s[depth] = own[: 2 * h, :].reshape(4, BLK, BLK)
+        v_ref[depth] = own[2 * h :, :]
+        for p, slot, lead in ((low, (depth + 3) % 4, 0), (high, (depth + 1) % 4, 2)):
+            d_s[slot, lead : lead + 2] = p[:h, :].reshape(two)
+            d_s[slot, 2 - lead : 4 - lead] = p[h + half : 2 * h + half, :].reshape(two)
+            v_ref[slot] = p[2 * h + half :, :]
+        slot = (depth + 2) % 4
+        for p, lead, first in ((far_low, 0, 0), (far_high, 2, half)):
+            d_s[slot, lead : lead + 2] = p[:h, :].reshape(two)
+            v_ref[slot, first : first + half, :] = p[h:, :]
         diag = tri_inverse_128([d_s[i, i] for i in range(4)])
         low10 = -nn(diag[1], nn(d_s[1, 0], diag[0]))
         low32 = -nn(diag[3], nn(d_s[3, 2], diag[2]))
@@ -250,11 +272,11 @@
         send[:, 2 * B :] = g2[theirs]
 
 
-def last_kernel(pos, f, u, a0, a1, a2, a3, others, f_ref, u_ref, t_s, h_s, s_s, src, dst):
+def last_kernel(pos, f, u, mine, others, f_ref, u_ref, t_s, h_s, s_s, src, dst):
     depth, core, base = pos[0], pos[1], pos[2]
-    for shift, mine in enumerate((a0, a1, a2, a3)):
+    for shift in range(4):
         slot = (depth + 4 - shift) % 4
-        t_s[slot * 2 + core] = mine[...]
+        t_s[slot * 2 + core] = mine[shift]
         t_s[slot * 2 + 1 - core] = others[shift]
     acc = jnp.where(iota((K, K), 0) == iota((K, K), 1), 1.0, 0.0)
     v = u[...]
@@ -438,15 +460,24 @@
     pos = pos.astype(jnp.int32)
     quarter, half = K // 4, K // 8
 
-    packed = (4 * BLK + quarter, BLK)
-    p0, p1, p2, p3, left_a, left_b = call(
-        pack_kernel, 8, [packed] * 4 + [(BLK, B)] * 2, [(K, BLK)], pos, factor, update
+    rows = 4 * BLK + quarter
+    own, up, down, left_a, left_b = call(
+        pack_kernel,
+        8,
+        [(rows, BLK), (rows + half, BLK), (rows + half, BLK), (BLK, B), (BLK, B)],
+        [(K, BLK)],
+        pos,
+        factor,
+        update,
     )
     left_a = move(left_a, [(owner(p, x), helper(p, x)) for p in (1, 2) for x in range(4)])
     left_b = move(left_b, [(owner(2, x), helper(2, x)) for x in range(4)])
-    parts, lefts = [p0], [left_a]
-    for s, p in ((1, p1), (2, p2), (3, p3)):
-        parts.append(move(p, depth_ring(s)))
+    lefts = [left_a]
+    low = move(up, depth_ring(1))
+    high = move(down, depth_ring(3))
+    part = 2 * BLK + half
+    far_low = move(low[:part], depth_ring(1))
+    far_high = move(high[:part], depth_ring(3))
     for s in range(1, 4):
         lefts.append(move(left_a, helper_ring(s)))
     rights = [left_b]
@@ -458,7 +489,11 @@
         [jax.ShapeDtypeStruct((3, B, B), jnp.bfloat16), (4, quarter, BLK), (quarter, B)],
         [(4, 4, BLK, BLK)],
         pos,
-        *parts,
+        own,
+        low,
+        high,
+        far_low,
+        far_high,
     )
     got1 = move(g0, [(owner(0, x), helper(1, x)) for x in range(4)])
     g0, got1 = lax.optimization_barrier((g0, got1))
@@ -478,13 +513,13 @@
     value = keep + move(send, swap + [(b, a) for a, b in swap])
     for moves in spread_steps():
         value = sum([move(value, pairs) for pairs in moves], value)
-    mine = [value] + [move(value, everywhere(s)) for s in range(1, 4)]
-    others = move(jnp.stack(mine), partner())
-    return tuple(last_call(pos, factor, update, *mine, others))
+    low, high = move(value, everywhere(1)), move(value, everywhere(3))
+    far = [move(low[: half // 2], everywhere(1)), move(high[half // 2 :], everywhere(3))]
+    mine = jnp.stack([value, low, jnp.concatenate(far, 0), high])
+    others = move(mine, partner())
+    return tuple(last_call(pos, factor, update, mine, others))
 
 
 def solution(mesh):
     spec = P(AXES, None)
-    return jax.shard_map(
-        steps, mesh=mesh, in_specs=(spec, spec), out_specs=(spec, spec), check_vma=False
-    )
+    return jax.shard_map(steps, mesh=mesh, in_specs=(spec, spec), out_specs=(spec, spec), check_vma=False)

time: 128 us -> 131 us (1.023)
  starting transfers between devices: 23 us -> 25.9 us
    ppermute x30 -> x32, starting transfers between devices: 23 us -> 25.9 us  [move(): return lax.ppermute(value, AXES, pairs)]
    ppermute x30 -> x32, waiting for transfers between devices: 62.4 us -> 61.8 us  [move(): return lax.ppermute(value, AXES, pairs)]
  transfers between devices with their start and end apart: 30 -> 32, of which waited for: 4 -> 4; matrix products, arithmetic and copies ran while one was open for 0% -> 0% of each run, Pallas kernels for 2% -> 2%
where the time goes in v3:
time: 131 us; the launch traced here: 130 us
  waiting for transfers between devices  61.8 us (47%)
  Pallas kernels  38.6 us (29%)
  starting transfers between devices  25.9 us (20%)
  local copies, waits for them, and re-layouts  2.17 us (2%)
    ppermute x32, waiting for transfers between devices, move(): return lax.ppermute(value, AXES, pairs)  61.8 us
    pallas_call x8, Pallas kernels, call(): pl.pallas_call(kernel, out_shape=outs, in_specs=[smem] + [vmem] * len(arr...  38.6 us
    ppermute x32, starting transfers between devices, move(): return lax.ppermute(value, AXES, pairs)  25.9 us
  transfers between devices with their start and end apart: 32, of which 4 were waited for; matrix products, arithmetic and copies ran while one was open for 0% of the time, Pallas kernels for 2%

profile of v3, /device:TPU:96, one launch (start us, length us, event | category | flops | bytes accessed | tf_op | source)
XLA Modules:
  0.0 129.9 jit_solution(10313514317491947052)
XLA Ops:
  0.7 0.1 stack.38.pos
  0.7 1.1 copy-done
  1.9 0.9 copy-done.2
  2.8 0.7 shard_map.41
  3.4 0.7 collective-permute-start
  4.1 0.7 collective-permute-start.1
  4.8 0.7 collective-permute-start.5
  5.5 0.7 collective-permute-start.2
  6.2 0.0 collective-permute-done.1.high
  6.2 0.7 collective-permute-start.3
  6.9 0.0 collective-permute-done.5.l0
  6.9 0.7 collective-permute-start.6
  7.6 0.7 collective-permute-start.7
  8.3 0.7 collective-permute-start.8
  9.0 0.7 collective-permute-start.12
  9.7 0.0 collective-permute-done.3.far_high
  9.7 0.6 shard_map.42
  10.2 0.7 collective-permute-start.4
  10.9 0.0 collective-permute-done.4.g
  10.9 0.0 collective-permute-done.6.l1
  11.0 0.0 collective-permute-done.8.l3
  11.0 0.6 shard_map.43
  11.5 0.7 collective-permute-start.9
  12.2 0.7 collective-permute-start.13
  12.9 0.7 collective-permute-start.14
  13.6 0.7 collective-permute-start.15
  14.3 0.7 collective-permute-start.11
  14.9 0.0 collective-permute-done.9.t
  15.0 0.6 shard_map.44
  15.5 0.7 collective-permute-start.10
  16.2 0.6 shard_map.45.t
  16.8 0.0 collective-permute-done.13.l1
  16.8 0.0 collective-permute-done.14.l2
  16.8 0.0 collective-permute-done.10.g.g1
  16.8 0.6 shard_map.46
  17.4 0.7 collective-permute-start.16
  18.0 0.0 collective-permute-done.16.t
  18.0 0.6 shard_map.47
  18.6 0.7 collective-permute-start.17
  19.3 0.0 collective-permute-done.17
  19.4 0.7 collective-permute-start.18
  20.0 0.7 collective-permute-start.19
  20.7 0.7 collective-permute-start.20
  21.4 0.0 collective-permute-done.19
  21.4 0.0 collective-permute-done.20
  21.5 0.7 collective-permute-start.21
  22.2 0.7 collective-permute-start.22
  22.8 0.7 collective-permute-start.23
  23.6 0.0 copy-start.1
  23.6 0.0 copy-start.3
  23.6 1.4 %collective-permute-start.24 = (f32[32,1536]{1,0:T(8,128)S(1)}, f32[32,1536]{1,0:T(8,128)S(1)}, u32[]{:S(2)}, u32[]{:S(2)}) collective-permute-start(f32[32,1536]{1,0:T(8,128)S(1)} %add_add_fusion.1), channel_id=1, source_target_pairs={{8,12},{9,13},{10,14},{11,15},{24,28},{25,29},{26,30},{27,31},{16,... | collective-permute-start | bytes 589832 | tf_op jit(solution)/shard_map/ppermute | solution.py:403
  25.1 0.7 collective-permute-start.25
  25.7 0.7 collective-permute-start.26
  26.4 52.3 %collective-permute-done.24 = f32[32,1536]{1,0:T(8,128)S(1)} collective-permute-done((f32[32,1536]{1,0:T(8,128)S(1)}, f32[32,1536]{1,0:T(8,128)S(1)}, u32[]{:S(2)}, u32[]{:S(2)}) %collective-permute-start.24) | collective-permute-done | bytes 196640 | tf_op jit(solution)/shard_map/ppermute | solution.py:403
  78.7 1.8 %collective-permute-start.27 = (f32[32,1536]{1,0:T(8,128)S(1)}, f32[32,1536]{1,0:T(8,128)S(1)}, u32[]{:S(2)}, u32[]{:S(2)}) collective-permute-start(f32[32,1536]{1,0:T(8,128)S(1)} %add_add_fusion), channel_id=1, source_target_pairs={{0,1},{1,2},{2,3},{3,0},{4,5},{5,6},{6,7},{7,4},{8,9},{9,10},{10,1... | collective-permute-start | bytes 589832 | tf_op jit(solution)/shard_map/ppermute | solution.py:403
  80.5 1.5 %collective-permute-start.29 = (f32[32,1536]{1,0:T(8,128)S(1)}, f32[32,1536]{1,0:T(8,128)S(1)}, u32[]{:S(2)}, u32[]{:S(2)}) collective-permute-start(f32[32,1536]{1,0:T(8,128)S(1)} %add_add_fusion), channel_id=1, source_target_pairs={{0,3},{1,0},{2,1},{3,2},{4,7},{5,4},{6,5},{7,6},{8,11},{9,8},{10,9... | collective-permute-start | bytes 589832 | tf_op jit(solution)/shard_map/ppermute | solution.py:403
  82.0 4.7 %collective-permute-done.27 = f32[32,1536]{1,0:T(8,128)S(1)} collective-permute-done((f32[32,1536]{1,0:T(8,128)S(1)}, f32[32,1536]{1,0:T(8,128)S(1)}, u32[]{:S(2)}, u32[]{:S(2)}) %collective-permute-start.27) | collective-permute-done | bytes 196640 | tf_op jit(solution)/shard_map/ppermute | solution.py:403
  86.8 0.8 collective-permute-start.28
  87.5 2.8 %collective-permute-start.30 = (f32[16,1536]{1,0:T(8,128)S(1)}, f32[16,1536]{1,0:T(8,128)S(1)}, u32[]{:S(2)}, u32[]{:S(2)}) collective-permute-start(f32[16,1536]{1,0:T(8,128)S(1)} %slice.19), channel_id=1, source_target_pairs={{0,3},{1,0},{2,1},{3,2},{4,7},{5,4},{6,5},{7,6},{8,11},{9,8},{10,9... | collective-permute-start | bytes 294920 | tf_op jit(solution)/shard_map/ppermute | solution.py:403
  90.3 2.5 %collective-permute-done.28 = f32[16,1536]{1,0:T(8,128)S(1)} collective-permute-done((f32[16,1536]{1,0:T(8,128)S(1)}, f32[16,1536]{1,0:T(8,128)S(1)}, u32[]{:S(2)}, u32[]{:S(2)}) %collective-permute-start.28) | collective-permute-done | bytes 98336 | tf_op jit(solution)/shard_map/ppermute | solution.py:403
  92.9 0.1 pad_maximum_fusion.mine
  92.9 0.1 collective-permute-start.31
  93.0 2.3 %collective-permute-done.31.others = f32[4,32,1536]{2,1,0:T(8,128)S(1)} collective-permute-done((f32[4,32,1536]{2,1,0:T(8,128)S(1)}, f32[4,32,1536]{2,1,0:T(8,128)S(1)}, u32[]{:S(2)}, u32[]{:S(2)}) %collective-permute-start.31) | collective-permute-done | bytes 786464 | tf_op jit(solution)/shard_map/ppermute | solution.py:403
  95.3 34.6 %shard_map.48 = (f32[128,1536]{1,0:T(8,128)}, f32[128,256]{1,0:T(8,128)}) custom-call(s32[5]{0:T(128)S(1)} %stack.38.pos, f32[128,1536]{1,0:T(8,128)S(1)} %copy-done.1, f32[128,256]{1,0:T(8,128)S(1)} %copy-done.3, f32[4,32,1536]{2,1,0:T(8,128)S(1)} %pad_maximum_fusion.mine, f32[4,32,1536]{2,1,0:T(8,128)S(1)} %collective-permute-done.31.others), custom_call_target="tpu_custom_call" | custom-call | tf_op jit(solution)/shard_map/pallas_call | solution.py:146
  (27 shorter events, 0.2 us)
Async XLA Ops:
  0.7 1.1 copy-start
  1.9 0.9 copy-start.2
  3.4 2.1 %collective-permute-start = (f32[608,128]{1,0:T(8,128)S(1)}, f32[608,128]{1,0:T(8,128)S(1)}, u32[]{:S(2)}, u32[]{:S(2)}) collective-permute-start(f32[608,128]{1,0:T(8,128)S(1)} %get-tuple-element.15), channel_id=1, source_target_pairs={{0,1},{1,2},{2,3},{3,0},{4,5},{5,6},{6,7},{7,4},{8,9},{9,10},{10,1... | collective-permute-start | bytes 933896 | tf_op jit(solution)/shard_map/ppermute | solution.py:403
  4.1 2.1 %collective-permute-start.1 = (f32[608,128]{1,0:T(8,128)S(1)}, f32[608,128]{1,0:T(8,128)S(1)}, u32[]{:S(2)}, u32[]{:S(2)}) collective-permute-start(f32[608,128]{1,0:T(8,128)S(1)} %get-tuple-element.16), channel_id=1, source_target_pairs={{0,3},{1,0},{2,1},{3,2},{4,7},{5,4},{6,5},{7,6},{8,11},{9,8},{10,9... | collective-permute-start | bytes 933896 | tf_op jit(solution)/shard_map/ppermute | solution.py:403
  4.8 2.1 %collective-permute-start.5 = (f32[128,512]{1,0:T(8,128)S(1)}, f32[128,512]{1,0:T(8,128)S(1)}, u32[]{:S(2)}, u32[]{:S(2)}) collective-permute-start(f32[128,512]{1,0:T(8,128)S(1)} %get-tuple-element.20), channel_id=1, source_target_pairs={{4,36},{5,37},{6,38},{7,39},{8,40},{9,41},{10,42},{11,43}} | collective-permute-start | bytes 786440 | tf_op jit(solution)/shard_map/ppermute | solution.py:403
  5.5 3.5 %collective-permute-start.2 = (f32[288,128]{1,0:T(8,128)S(1)}, f32[288,128]{1,0:T(8,128)S(1)}, u32[]{:S(2)}, u32[]{:S(2)}) collective-permute-start(f32[288,128]{1,0:T(8,128)S(1)} %slice.16), channel_id=1, source_target_pairs={{0,1},{1,2},{2,3},{3,0},{4,5},{5,6},{6,7},{7,4},{8,9},{9,10},{10,1... | collective-permute-start | bytes 442376 | tf_op jit(solution)/shard_map/ppermute | solution.py:403
  6.2 3.4 %collective-permute-start.3 = (f32[288,128]{1,0:T(8,128)S(1)}, f32[288,128]{1,0:T(8,128)S(1)}, u32[]{:S(2)}, u32[]{:S(2)}) collective-permute-start(f32[288,128]{1,0:T(8,128)S(1)} %slice.17), channel_id=1, source_target_pairs={{0,3},{1,0},{2,1},{3,2},{4,7},{5,4},{6,5},{7,6},{8,11},{9,8},{10,9... | collective-permute-start | bytes 442376 | tf_op jit(solution)/shard_map/ppermute | solution.py:403
  6.9 4.0 %collective-permute-start.6 = (f32[128,512]{1,0:T(8,128)S(1)}, f32[128,512]{1,0:T(8,128)S(1)}, u32[]{:S(2)}, u32[]{:S(2)}) collective-permute-start(f32[128,512]{1,0:T(8,128)S(1)} %collective-permute-done.5.l0), channel_id=1, source_target_pairs={{36,37},{37,38},{38,39},{39,36},{40,41},{41,42},{42,43},{43,40}} | collective-permute-start | bytes 786440 | tf_op jit(solution)/shard_map/ppermute | solution.py:403
  7.6 3.3 %collective-permute-start.7 = (f32[128,512]{1,0:T(8,128)S(1)}, f32[128,512]{1,0:T(8,128)S(1)}, u32[]{:S(2)}, u32[]{:S(2)}) collective-permute-start(f32[128,512]{1,0:T(8,128)S(1)} %collective-permute-done.5.l0), channel_id=1, source_target_pairs={{36,38},{37,39},{38,36},{39,37},{40,42},{41,43},{42,40},{43,41}} | collective-permute-start | bytes 786440 | tf_op jit(solution)/shard_map/ppermute | solution.py:403
  8.3 2.7 %collective-permute-start.8 = (f32[128,512]{1,0:T(8,128)S(1)}, f32[128,512]{1,0:T(8,128)S(1)}, u32[]{:S(2)}, u32[]{:S(2)}) collective-permute-start(f32[128,512]{1,0:T(8,128)S(1)} %collective-permute-done.5.l0), channel_id=1, source_target_pairs={{36,39},{37,36},{38,37},{39,38},{40,43},{41,40},{42,41},{43,42}} | collective-permute-start | bytes 786440 | tf_op jit(solution)/shard_map/ppermute | solution.py:403
  9.0 3.2 %collective-permute-start.12 = (f32[128,512]{1,0:T(8,128)S(1)}, f32[128,512]{1,0:T(8,128)S(1)}, u32[]{:S(2)}, u32[]{:S(2)}) collective-permute-start(f32[128,512]{1,0:T(8,128)S(1)} %get-tuple-element.23), channel_id=1, source_target_pairs={{8,40},{9,41},{10,42},{11,43}} | collective-permute-start | bytes 786440 | tf_op jit(solution)/shard_map/ppermute | solution.py:403
  10.2 0.7 collective-permute-start.4
  11.5 3.4 %collective-permute-start.9 = (f32[4,64,128]{2,1,0:T(8,128)S(1)}, f32[4,64,128]{2,1,0:T(8,128)S(1)}, u32[]{:S(2)}, u32[]{:S(2)}) collective-permute-start(f32[4,64,128]{2,1,0:T(8,128)S(1)} %shard_map.43), channel_id=1, source_target_pairs={{36,4},{37,5},{38,6},{39,7}} | collective-permute-start | bytes 393224 | tf_op jit(solution)/shard_map/ppermute | solution.py:403
  12.2 4.5 %collective-permute-start.13 = (f32[128,512]{1,0:T(8,128)S(1)}, f32[128,512]{1,0:T(8,128)S(1)}, u32[]{:S(2)}, u32[]{:S(2)}) collective-permute-start(f32[128,512]{1,0:T(8,128)S(1)} %collective-permute-done.12.l0), channel_id=1, source_target_pairs={{40,41},{41,42},{42,43},{43,40}} | collective-permute-start | bytes 786440 | tf_op jit(solution)/shard_map/ppermute | solution.py:403
  12.9 3.9 %collective-permute-start.14 = (f32[128,512]{1,0:T(8,128)S(1)}, f32[128,512]{1,0:T(8,128)S(1)}, u32[]{:S(2)}, u32[]{:S(2)}) collective-permute-start(f32[128,512]{1,0:T(8,128)S(1)} %collective-permute-done.12.l0), channel_id=1, source_target_pairs={{40,42},{41,43},{42,40},{43,41}} | collective-permute-start | bytes 786440 | tf_op jit(solution)/shard_map/ppermute | solution.py:403
  13.6 3.2 %collective-permute-start.15 = (f32[128,512]{1,0:T(8,128)S(1)}, f32[128,512]{1,0:T(8,128)S(1)}, u32[]{:S(2)}, u32[]{:S(2)}) collective-permute-start(f32[128,512]{1,0:T(8,128)S(1)} %collective-permute-done.12.l0), channel_id=1, source_target_pairs={{40,43},{41,40},{42,41},{43,42}} | collective-permute-start | bytes 786440 | tf_op jit(solution)/shard_map/ppermute | solution.py:403
  14.3 1.9 %collective-permute-start.11 = (f32[64,512]{1,0:T(8,128)S(1)}, f32[64,512]{1,0:T(8,128)S(1)}, u32[]{:S(2)}, u32[]{:S(2)}) collective-permute-start(f32[64,512]{1,0:T(8,128)S(1)} %get-tuple-element.22), channel_id=1, source_target_pairs={{0,40},{1,41},{2,42},{3,43}} | collective-permute-start | bytes 393224 | tf_op jit(solution)/shard_map/ppermute | solution.py:403
  15.5 1.3 collective-permute-start.10
  17.4 0.7 collective-permute-start.16
  18.6 0.7 collective-permute-start.17
  19.4 2.0 %collective-permute-start.18 = (f32[32,1536]{1,0:T(8,128)S(1)}, f32[32,1536]{1,0:T(8,128)S(1)}, u32[]{:S(2)}, u32[]{:S(2)}) collective-permute-start(f32[32,1536]{1,0:T(8,128)S(1)} %add.44), channel_id=1, source_target_pairs={{8,24},{9,25},{10,26},{11,27},{40,168},{41,169},{42,170},{43,171}} | collective-permute-start | bytes 589832 | tf_op jit(solution)/shard_map/ppermute | solution.py:403
  20.0 1.4 %collective-permute-start.19 = (f32[32,1536]{1,0:T(8,128)S(1)}, f32[32,1536]{1,0:T(8,128)S(1)}, u32[]{:S(2)}, u32[]{:S(2)}) collective-permute-start(f32[32,1536]{1,0:T(8,128)S(1)} %add.44), channel_id=1, source_target_pairs={{8,16},{9,17},{10,18},{11,19},{40,104},{41,105},{42,106},{43,107}} | collective-permute-start | bytes 589832 | tf_op jit(solution)/shard_map/ppermute | solution.py:403
  20.7 0.7 collective-permute-start.20
  21.5 2.0 %collective-permute-start.21 = (f32[32,1536]{1,0:T(8,128)S(1)}, f32[32,1536]{1,0:T(8,128)S(1)}, u32[]{:S(2)}, u32[]{:S(2)}) collective-permute-start(f32[32,1536]{1,0:T(8,128)S(1)} %add_add_fusion.2), channel_id=1, source_target_pairs={{8,136},{9,137},{10,138},{11,139},{24,152},{25,153},{26,154},{27,1... | collective-permute-start | bytes 589832 | tf_op jit(solution)/shard_map/ppermute | solution.py:403
  22.2 1.4 %collective-permute-start.22 = (f32[32,1536]{1,0:T(8,128)S(1)}, f32[32,1536]{1,0:T(8,128)S(1)}, u32[]{:S(2)}, u32[]{:S(2)}) collective-permute-start(f32[32,1536]{1,0:T(8,128)S(1)} %add_add_fusion.2), channel_id=1, source_target_pairs={{8,72},{9,73},{10,74},{11,75},{24,88},{25,89},{26,90},{27,91},{16,... | collective-permute-start | bytes 589832 | tf_op jit(solution)/shard_map/ppermute | solution.py:403
  22.8 0.7 collective-permute-start.23
  23.6 71.7 %copy-start.1 = (f32[128,1536]{1,0:T(8,128)S(1)}, f32[128,1536]{1,0:T(8,128)}, u32[]{:S(2)}) copy-start(f32[128,1536]{1,0:T(8,128)} %f.3) | copy-start | bytes 2359300
  23.6 71.7 %copy-start.3 = (f32[128,256]{1,0:T(8,128)S(1)}, f32[128,256]{1,0:T(8,128)}, u32[]{:S(2)}) copy-start(f32[128,256]{1,0:T(8,128)} %u.3) | copy-start | bytes 393220
  23.6 55.0 %collective-permute-start.24 = (f32[32,1536]{1,0:T(8,128)S(1)}, f32[32,1536]{1,0:T(8,128)S(1)}, u32[]{:S(2)}, u32[]{:S(2)}) collective-permute-start(f32[32,1536]{1,0:T(8,128)S(1)} %add_add_fusion.1), channel_id=1, source_target_pairs={{8,12},{9,13},{10,14},{11,15},{24,28},{25,29},{26,30},{27,31},{16,... | collective-permute-start | bytes 589832 | tf_op jit(solution)/shard_map/ppermute | solution.py:403
  25.1 53.6 %collective-permute-start.25 = (f32[32,1536]{1,0:T(8,128)S(1)}, f32[32,1536]{1,0:T(8,128)S(1)}, u32[]{:S(2)}, u32[]{:S(2)}) collective-permute-start(f32[32,1536]{1,0:T(8,128)S(1)} %add_add_fusion.1), channel_id=1, source_target_pairs={{40,48},{41,49},{42,50},{43,51},{168,176},{169,177},{170,178},{171... | collective-permute-start | bytes 589832 | tf_op jit(solution)/shard_map/ppermute | solution.py:403
  25.7 52.9 %collective-permute-start.26 = (f32[32,1536]{1,0:T(8,128)S(1)}, f32[32,1536]{1,0:T(8,128)S(1)}, u32[]{:S(2)}, u32[]{:S(2)}) collective-permute-start(f32[32,1536]{1,0:T(8,128)S(1)} %add_add_fusion.1), channel_id=1, source_target_pairs={{40,32},{41,33},{42,34},{43,35},{168,160},{169,161},{170,162},{171... | collective-permute-start | bytes 589832 | tf_op jit(solution)/shard_map/ppermute | solution.py:403
  78.7 8.0 %collective-permute-start.27 = (f32[32,1536]{1,0:T(8,128)S(1)}, f32[32,1536]{1,0:T(8,128)S(1)}, u32[]{:S(2)}, u32[]{:S(2)}) collective-permute-start(f32[32,1536]{1,0:T(8,128)S(1)} %add_add_fusion), channel_id=1, source_target_pairs={{0,1},{1,2},{2,3},{3,0},{4,5},{5,6},{6,7},{7,4},{8,9},{9,10},{10,1... | collective-permute-start | bytes 589832 | tf_op jit(solution)/shard_map/ppermute | solution.py:403
  80.5 7.0 %collective-permute-start.29 = (f32[32,1536]{1,0:T(8,128)S(1)}, f32[32,1536]{1,0:T(8,128)S(1)}, u32[]{:S(2)}, u32[]{:S(2)}) collective-permute-start(f32[32,1536]{1,0:T(8,128)S(1)} %add_add_fusion), channel_id=1, source_target_pairs={{0,3},{1,0},{2,1},{3,2},{4,7},{5,4},{6,5},{7,6},{8,11},{9,8},{10,9... | collective-permute-start | bytes 589832 | tf_op jit(solution)/shard_map/ppermute | solution.py:403
  86.8 6.1 %collective-permute-start.28 = (f32[16,1536]{1,0:T(8,128)S(1)}, f32[16,1536]{1,0:T(8,128)S(1)}, u32[]{:S(2)}, u32[]{:S(2)}) collective-permute-start(f32[16,1536]{1,0:T(8,128)S(1)} %slice.18), channel_id=1, source_target_pairs={{0,1},{1,2},{2,3},{3,0},{4,5},{5,6},{6,7},{7,4},{8,9},{9,10},{10,1... | collective-permute-start | bytes 294920 | tf_op jit(solution)/shard_map/ppermute | solution.py:403
  87.5 5.3 %collective-permute-start.30 = (f32[16,1536]{1,0:T(8,128)S(1)}, f32[16,1536]{1,0:T(8,128)S(1)}, u32[]{:S(2)}, u32[]{:S(2)}) collective-permute-start(f32[16,1536]{1,0:T(8,128)S(1)} %slice.19), channel_id=1, source_target_pairs={{0,3},{1,0},{2,1},{3,2},{4,7},{5,4},{6,5},{7,6},{8,11},{9,8},{10,9... | collective-permute-start | bytes 294920 | tf_op jit(solution)/shard_map/ppermute | solution.py:403
  92.9 2.4 %collective-permute-start.31 = (f32[4,32,1536]{2,1,0:T(8,128)S(1)}, f32[4,32,1536]{2,1,0:T(8,128)S(1)}, u32[]{:S(2)}, u32[]{:S(2)}) collective-permute-start(f32[4,32,1536]{2,1,0:T(8,128)S(1)} %pad_maximum_fusion.mine), channel_id=1, source_target_pairs={{0,32},{32,0},{4,36},{36,4},{64,96},{96,64},{68,100},{100,68},{128... | collective-permute-start | bytes 2359304 | tf_op jit(solution)/shard_map/ppermute | solution.py:403
